TPU v7x, 32 devices: a 4x2x2 block of a 4x4x8 slice. The times are simulated.
32 devices in a mesh: dp: 4 (over y, z), sp: 8 (over x, core).
Axes of the slice: x: 4, y: 2, z: 2, core: 2. Of those that a mesh axis runs over, the one named last changes fastest.
The devices are a block of a 4x4x8 slice.
Arguments:
- hidden: bfloat16 [64, 128, 2048], P('dp', 'sp'), parts along dimension 0
- attn_norm: bfloat16 [2048], replicated
- w_q: bfloat16 [2048, 32, 64], replicated
- w_k: bfloat16 [2048, 8, 64], replicated
- w_v: bfloat16 [2048, 8, 64], replicated
- w_o: bfloat16 [32, 64, 2048], replicated
- mlp_norm: bfloat16 [2048], replicated
- w_gate: bfloat16 [2048, 8192], replicated
- w_up: bfloat16 [2048, 8192], replicated
- w_down: bfloat16 [8192, 2048], replicated
- mamba_norm: bfloat16 [2048], replicated
- w_in_x: bfloat16 [2048, 4096], replicated
- w_in_z: bfloat16 [2048, 4096], replicated
- conv_w: bfloat16 [4, 4096], replicated
- conv_b: bfloat16 [4096], replicated
- w_xproj: bfloat16 [4096, 160], replicated
- dt_norm: float32 [128], replicated
- b_norm: float32 [16], replicated
- c_norm: float32 [16], replicated
- w_dt: bfloat16 [128, 4096], replicated
- dt_bias: float32 [4096], replicated
- a_log: float32 [4096, 16], replicated
- d_skip: float32 [4096], replicated
- w_out: bfloat16 [4096, 2048], replicated
Outputs:
- output: bfloat16 [64, 128, 2048], P('dp', 'sp'), parts along dimension 0
There are 4 independent parts. A program takes and returns all parts, laid end to end along the dimension named above; an argument that names none is the same for every part.
All inputs are finite; a program needn't handle non-finite values.
Results may differ from a plain program's by a relative error of at most 0.02.
Values are sent between devices in bfloat16 or wider.
A program may use at most 768 MiB of HBM per device.

v0:
```python
import functools
import jax
import jax.numpy as jnp
from jax import lax
from jax.sharding import PartitionSpec as P

EPS = 1e-6
CONV = 4


def rms_scale(values, gain_vec):
    values_f = values.astype(jnp.float32)
    inv_rms = lax.rsqrt(jnp.mean(values_f * values_f, axis=-1, keepdims=True) + EPS)
    return values_f * inv_rms * gain_vec.astype(jnp.float32)


def attention_layer(hidden, attn_norm, w_q, w_k, w_v, w_o):
    n_batch, tok_local, model_dim = hidden.shape
    n_heads, head_dim = w_q.shape[1], w_q.shape[2]
    kv_heads = w_k.shape[1]
    groups = n_heads // kv_heads
    normed = rms_scale(hidden, attn_norm).astype(jnp.bfloat16).reshape(n_batch * tok_local, model_dim)
    queries = jnp.dot(normed, w_q.reshape(model_dim, n_heads * head_dim), preferred_element_type=jnp.float32)
    queries = queries.astype(jnp.bfloat16).reshape(n_batch, tok_local, kv_heads, groups, head_dim)
    key_proj = jnp.dot(normed, w_k.reshape(model_dim, kv_heads * head_dim), preferred_element_type=jnp.float32)
    key_proj = key_proj.astype(jnp.bfloat16).reshape(n_batch, tok_local, kv_heads, head_dim)
    val_proj = jnp.dot(normed, w_v.reshape(model_dim, kv_heads * head_dim), preferred_element_type=jnp.float32)
    val_proj = val_proj.astype(jnp.bfloat16).reshape(n_batch, tok_local, kv_heads, head_dim)
    queries = lax.all_to_all(queries, "sp", 2, 1, tiled=True)
    key_proj = lax.all_to_all(key_proj, "sp", 2, 1, tiled=True)
    val_proj = lax.all_to_all(val_proj, "sp", 2, 1, tiled=True)
    seq_len = key_proj.shape[1]
    causal = lax.broadcasted_iota(jnp.int32, (seq_len, 1), 0) >= lax.broadcasted_iota(jnp.int32, (1, seq_len), 1)
    scores = jnp.einsum("bqngd,bsnd->bngqs", queries, key_proj, preferred_element_type=jnp.float32) * head_dim ** -0.5
    scores = jnp.where(causal, scores, -jnp.inf)
    attn_prob = jax.nn.softmax(scores, axis=-1).astype(jnp.bfloat16)
    attn_out = jnp.einsum("bngqs,bsnd->bqngd", attn_prob, val_proj, preferred_element_type=jnp.float32).astype(jnp.bfloat16)
    attn_out = lax.all_to_all(attn_out, "sp", 1, 2, tiled=True)
    proj_out = jnp.dot(attn_out.reshape(n_batch * tok_local, n_heads * head_dim), w_o.reshape(n_heads * head_dim, model_dim), preferred_element_type=jnp.float32)
    return (hidden.astype(jnp.float32) + proj_out.reshape(n_batch, tok_local, model_dim)).astype(jnp.bfloat16)


def mlp_layer(hidden, mlp_norm, w_gate, w_up, w_down):
    model_dim = hidden.shape[-1]
    normed = rms_scale(hidden, mlp_norm).astype(jnp.bfloat16).reshape(-1, model_dim)
    gate_pre = jnp.dot(normed, w_gate, preferred_element_type=jnp.float32)
    up_proj = jnp.dot(normed, w_up, preferred_element_type=jnp.float32)
    act_val = (jax.nn.silu(gate_pre) * up_proj).astype(jnp.bfloat16)
    down_out = jnp.dot(act_val, w_down, preferred_element_type=jnp.float32)
    return (hidden.astype(jnp.float32) + down_out.reshape(hidden.shape)).astype(jnp.bfloat16)


def mamba_mixer(hidden, mamba_norm, w_in_x, w_in_z, conv_w, conv_b, w_xproj, dt_norm, b_norm, c_norm, w_dt, dt_bias, a_log, d_skip, w_out, n_shards):
    n_batch, tok_local, model_dim = hidden.shape
    n_inner, n_state = a_log.shape
    dt_rank = w_dt.shape[0]
    normed = rms_scale(hidden, mamba_norm).astype(jnp.bfloat16)
    x_inner = jnp.einsum("btd,de->tbe", normed, w_in_x, preferred_element_type=jnp.float32).astype(jnp.bfloat16)
    z_gate = jnp.einsum("btd,de->tbe", normed, w_in_z, preferred_element_type=jnp.float32).astype(jnp.bfloat16)
    shard_idx = lax.axis_index("sp")
    halo_rows = lax.ppermute(x_inner[tok_local - (CONV - 1):], "sp", [(src_idx, src_idx + 1) for src_idx in range(n_shards - 1)])
    padded = jnp.concatenate([halo_rows, x_inner], axis=0)
    conv_acc = conv_b.astype(jnp.float32)
    for tap_idx in range(CONV):
        conv_acc = conv_acc + padded[tap_idx:tap_idx + tok_local].astype(jnp.float32) * conv_w[tap_idx].astype(jnp.float32)
    x_conv = jax.nn.silu(conv_acc).astype(jnp.bfloat16)
    x_dbl = jnp.einsum("tbe,er->tbr", x_conv, w_xproj, preferred_element_type=jnp.float32)
    dt_in = rms_scale(x_dbl[..., :dt_rank], dt_norm).astype(jnp.bfloat16)
    b_mat = rms_scale(x_dbl[..., dt_rank:dt_rank + n_state], b_norm)
    c_mat = rms_scale(x_dbl[..., dt_rank + n_state:], c_norm)
    step_size = jax.nn.softplus(jnp.einsum("tbr,re->tbe", dt_in, w_dt, preferred_element_type=jnp.float32) + dt_bias)
    a_mat = -jnp.exp(a_log)

    def local_step(ssm_state, inputs):
        step_t, x_t, b_t, c_t = inputs
        decay_t = jnp.exp(step_t[:, :, None] * a_mat)
        ssm_state = decay_t * ssm_state + (step_t * x_t.astype(jnp.float32))[:, :, None] * b_t[:, None, :]
        return ssm_state, jnp.sum(ssm_state * c_t[:, None, :], axis=-1)

    def carry_step(ssm_state, inputs):
        step_t, c_t = inputs
        ssm_state = jnp.exp(step_t[:, :, None] * a_mat) * ssm_state
        return ssm_state, jnp.sum(ssm_state * c_t[:, None, :], axis=-1)

    zero_state = jnp.zeros((n_batch, n_inner, n_state), jnp.float32)
    end_state, y_local = lax.scan(local_step, zero_state, (step_size, x_conv, b_mat, c_mat))
    step_total = jnp.sum(step_size, axis=0)
    all_states = lax.all_gather(end_state, "sp")
    all_totals = lax.all_gather(step_total, "sp")
    preceding = jnp.arange(n_shards) < shard_idx
    prec_mask = preceding[:, None, None]
    before_total = jnp.sum(jnp.where(prec_mask, all_totals, 0.0), axis=0)
    gap_sum = jnp.where(prec_mask, before_total[None] - jnp.cumsum(all_totals, axis=0), 0.0)
    carry_weight = jnp.where(preceding[:, None, None, None], jnp.exp(gap_sum[..., None] * a_mat), 0.0)
    start_state = jnp.sum(carry_weight * all_states, axis=0)
    y_carry = lax.scan(carry_step, start_state, (step_size, c_mat))[1]
    y_total = y_local + y_carry + d_skip * x_conv.astype(jnp.float32)
    gated_y = (y_total * jax.nn.silu(z_gate.astype(jnp.float32))).astype(jnp.bfloat16)
    mamba_out = jnp.einsum("tbe,ed->btd", gated_y, w_out, preferred_element_type=jnp.float32)
    return (hidden.astype(jnp.float32) + mamba_out).astype(jnp.bfloat16)


def layer_pair(hidden, attn_norm, w_q, w_k, w_v, w_o, mlp_norm, w_gate, w_up, w_down, mamba_norm, w_in_x, w_in_z, conv_w, conv_b, w_xproj, dt_norm, b_norm, c_norm, w_dt, dt_bias, a_log, d_skip, w_out, n_shards):
    after_attn = attention_layer(hidden, attn_norm, w_q, w_k, w_v, w_o)
    after_mlp = mlp_layer(after_attn, mlp_norm, w_gate, w_up, w_down)
    return mamba_mixer(after_mlp, mamba_norm, w_in_x, w_in_z, conv_w, conv_b, w_xproj, dt_norm, b_norm, c_norm, w_dt, dt_bias, a_log, d_skip, w_out, n_shards)


def solution(mesh):
    act_spec = P("dp", "sp", None)
    return jax.shard_map(
        functools.partial(layer_pair, n_shards=mesh.shape["sp"]),
        mesh=mesh,
        in_specs=(act_spec,) + (P(),) * 23,
        out_specs=act_spec,
        check_vma=False,
    )
```

profile of v0, /device:TPU:81, one launch (start us, length us, event | category | flops | bytes accessed | tf_op | source)
XLA Modules:
  0.0 813.5 jit_solution(10206837330365724601)
XLA Ops:
  12.7 6.0 all-to-all-start.1
  30.0 6.1 convolution_convert_fusion
  45.4 5.5 all-to-all-start.2
  54.4 11.1 %all-to-all-done.2 = bf16[8,2,32768]{2,1,0:T(2,128)(2,1)S(1)} async-done(((bf16[8,2,32768]{2,1,0:T(2,128)(2,1)}), bf16[8,2,32768]{2,1,0:T(2,128)(2,1)S(1)}, u32[]{:S(2)}, u32[]{:S(2)}) %all-to-all-start.2) | async-done | bytes 1048608 | tf_op jit(solution)/shard_map/all_to_all | solution.py:29
  80.9 14.6 %all-to-all-done.3 = bf16[8,2,32768]{2,1,0:T(2,128)(2,1)S(1)} async-done(((bf16[8,2,32768]{2,1,0:T(2,128)(2,1)}), bf16[8,2,32768]{2,1,0:T(2,128)(2,1)S(1)}, u32[]{:S(2)}, u32[]{:S(2)}) %all-to-all-start.3) | async-done | bytes 1048608 | tf_op jit(solution)/shard_map/all_to_all | solution.py:38
  108.8 6.2 fusion.53
  115.4 17.0 %fusion.93 = f32[256,8192]{1,0:T(8,128)} fusion(bf16[256,2048]{1,0:T(8,128)(2,1)S(1)} %bitcast.223, bf16[2048,8192]{1,0:T(8,128)(2,1)} %param.35), kind=kOutput, calls=%fused_computation.119 | convolution fusion | flops 8589934592 | bytes 42991616 | tf_op jit(solution)/shard_map/dot_general | solution.py:46
  132.4 29.5 %fusion.8 = f32[256,2048]{1,0:T(8,128)} fusion(bf16[8192,2048]{1,0:T(8,128)(2,1)} %param.37, bf16[256,2048]{1,0:T(8,128)(2,1)S(1)} %bitcast.224, bf16[2048,8192]{1,0:T(8,128)(2,1)} %param.36, f32[256,8192]{1,0:T(8,128)} %fusion.93), kind=kOutput, calls=%fused_computation.21 | convolution fusion | flops 17192452096 | bytes 78643200 | tf_op jit(solution)/shard_map/dot_general | solution.py:49
  163.9 8.9 %fusion.24 = bf16[16,16,4096]{2,0,1:T(8,128)(2,1)S(1)} fusion(bf16[2048,4096]{1,0:T(8,128)(2,1)} %param.39, bf16[16,16,2048]{2,1,0:T(8,128)(2,1)S(1)} %get-tuple-element.203, f32[2048]{0:T(1024)S(1)} %convert_element_type.174, f32[16,16]{1,0:T(8,128)S(1)} %add_rsqrt_fusion.3), kind=kOutput, calls=%fused_computation.31 | convolution fusion | flops 4298113024 | bytes 19932160 | tf_op jit(solution)/shard_map/btd,de->tbe/dot_general | solution.py:58
  177.9 6.0 collective-permute-done
  183.9 7.0 multiply_convert_fusion.1
  196.9 5.5 fusion.92
  205.5 204.9 %while.26 = (s32[]{:T(128)}, f32[16,4096,16]{1,2,0:T(8,128)}, f32[16,16,4096]{2,0,1:T(8,128)}, f32[16,16,4096]{2,1,0:T(8,128)}, f32[4096,16]{0,1:T(8,128)S(1)}, ...) while((s32[]{:T(128)}, f32[16,4096,16]{1,2,0:T(8,128)}, ...), condition=%wide.region_10.11_spmd.clone, body=%wide.region_8.10_spmd.clone.sunk | while | flops 7405571 | bytes 11671683 | solution.py:86
  211.3 6.0 dynamic_update_slice.11
  224.2 6.0 dynamic_update_slice.11
  237.1 6.0 dynamic_update_slice.11
  249.9 6.0 dynamic_update_slice.11
  262.8 6.0 dynamic_update_slice.11
  275.7 6.0 dynamic_update_slice.11
  288.6 6.0 dynamic_update_slice.11
  301.4 6.0 dynamic_update_slice.11
  314.3 6.0 dynamic_update_slice.11
  327.2 6.0 dynamic_update_slice.11
  340.1 6.0 dynamic_update_slice.11
  352.9 6.0 dynamic_update_slice.11
  365.8 6.0 dynamic_update_slice.11
  378.7 6.0 dynamic_update_slice.11
  391.6 6.0 dynamic_update_slice.11
  404.5 6.0 dynamic_update_slice.11
  415.6 152.0 %all-gather.7.cloned.1.call-done = f32[128,4096,16]{1,2,0:T(8,128)} async-done(((f32[16,4096,16]{1,2,0:T(8,128)}), f32[128,4096,16]{1,2,0:T(8,128)}) %all-gather.7.cloned.1.call-update) | async-done | bytes 33554448 | tf_op jit(solution)/shard_map/all_gather | solution.py:88
  567.6 17.1 %multiply_reduce_fusion.2 = f32[16,4096,16]{1,2,0:T(8,128)} fusion(f32[8,16,4096,16]{2,3,1,0:T(8,128)} %bitcast.206, f32[4096,16]{0,1:T(8,128)S(1)} %get-tuple-element.368, f32[8,16,4096]{2,1,0:T(8,128)} %fusion.27, pred[8]{0:T(512)(128)(4,1)S(1)} %iota_compare_fusion.1), kind=kLoop, calls=%fused_computation.11 | loop fusion | flops 32505856 | bytes 40108040 | tf_op jit(solution)/shard_map/reduce_sum | solution.py:95
  587.1 199.6 %while.25 = (s32[]{:T(128)}, f32[16,4096,16]{1,2,0:T(8,128)}, f32[16,16,4096]{2,0,1:T(8,128)}, f32[16,16,4096]{2,1,0:T(8,128)}, f32[4096,16]{0,1:T(8,128)S(1)}, ...) while((s32[]{:T(128)}, f32[16,4096,16]{1,2,0:T(8,128)}, f32[16,16,4096]{2,0,1:T(8,128)}, ...), condition=%wide.region_17.18_spmd, body=%wide.region_15.17_spmd.sunk | while | flops 4128770 | bytes 10751073 | solution.py:96
  588.1 5.2 multiply_reduce_fusion.8
  593.6 6.0 dynamic_update_slice.10
  600.6 5.2 multiply_reduce_fusion.8
  606.1 6.0 dynamic_update_slice.10
  613.1 5.2 multiply_reduce_fusion.8
  618.6 6.0 dynamic_update_slice.10
  625.6 5.2 multiply_reduce_fusion.8
  631.1 6.0 dynamic_update_slice.10
  638.1 5.2 multiply_reduce_fusion.8
  643.6 6.0 dynamic_update_slice.10
  650.6 5.2 multiply_reduce_fusion.8
  656.1 6.0 dynamic_update_slice.10
  663.1 5.2 multiply_reduce_fusion.8
  668.6 6.0 dynamic_update_slice.10
  675.6 5.2 multiply_reduce_fusion.8
  681.1 6.0 dynamic_update_slice.10
  688.1 5.2 multiply_reduce_fusion.8
  693.6 6.0 dynamic_update_slice.10
  700.5 5.2 multiply_reduce_fusion.8
  706.0 6.0 dynamic_update_slice.10
  713.0 5.2 multiply_reduce_fusion.8
  718.5 6.0 dynamic_update_slice.10
  725.4 5.2 multiply_reduce_fusion.8
  730.9 6.0 dynamic_update_slice.10
  737.9 5.2 multiply_reduce_fusion.8
  743.4 6.0 dynamic_update_slice.10
  750.3 5.2 multiply_reduce_fusion.8
  755.8 6.0 dynamic_update_slice.10
  762.8 5.2 multiply_reduce_fusion.8
  768.3 6.0 dynamic_update_slice.10
  780.7 6.0 dynamic_update_slice.10
  786.7 19.8 %fusion.45 = bf16[16,16,2048]{2,1,0:T(8,128)(2,1)} fusion(bf16[4096,2048]{1,0:T(8,128)(2,1)} %param.51, bf16[16,16,4096]{2,0,1:T(8,128)(2,1)} %copy-done.2, f32[16,16,4096]{2,0,1:T(8,128)} %get-tuple-element.80, f32[16,16,4096]{2,0,1:T(8,128)} %get-tuple-element.82, bf16[2048,4096]{1,0:T(8,128)(2,1)} %param.40, bf16[16,16,2048]{2,1,0:T(8,128)(2,1)S(1)} %copy-done.8, ...), kind=kOutput, calls=%fused_computation.57 | convolution fusion | flops 8606187520 | bytes 46162944 | tf_op jit(solution)/shard_map/tbe,ed->btd/dot_general | solution.py:99
  (263 shorter events, 216.3 us)
Async XLA Ops:
  6.5 3.9 copy-start
  10.4 10.6 %copy-start.6 = (bf16[16,16,2048]{2,1,0:T(8,128)(2,1)}, bf16[16,16,2048]{2,1,0:T(8,128)(2,1)S(1)}, u32[]{:S(2)}) copy-start(bf16[16,16,2048]{2,1,0:T(8,128)(2,1)S(1)} %fusion.52) | copy-start | bytes 3145732
  12.7 12.3 %all-to-all-start.1 = ((bf16[8,2,8192]{2,1,0:T(2,128)(2,1)}), bf16[8,2,8192]{2,1,0:T(2,128)(2,1)S(1)}, u32[]{:S(2)}, u32[]{:S(2)}) async-start(bf16[8,2,8192]{2,1,0:T(2,128)(2,1)} %reshape.224), calls=%async_computation.1 | async-start | bytes 524288 | tf_op jit(solution)/shard_map/all_to_all | solution.py:30
  25.0 20.4 %all-to-all-start = ((bf16[8,2,8192]{2,1,0:T(2,128)(2,1)}), bf16[8,2,8192]{2,1,0:T(2,128)(2,1)}, u32[]{:S(2)}, u32[]{:S(2)}) async-start(bf16[8,2,8192]{2,1,0:T(2,128)(2,1)} %reshape.222), calls=%async_computation | async-start | bytes 524288 | tf_op jit(solution)/shard_map/all_to_all | solution.py:31
  45.4 20.2 %all-to-all-start.2 = ((bf16[8,2,32768]{2,1,0:T(2,128)(2,1)}), bf16[8,2,32768]{2,1,0:T(2,128)(2,1)S(1)}, u32[]{:S(2)}, u32[]{:S(2)}) async-start(bf16[8,2,32768]{2,1,0:T(2,128)(2,1)} %reshape.226), calls=%async_computation.2 | async-start | bytes 2097152 | tf_op jit(solution)/shard_map/all_to_all | solution.py:29
  67.0 1.0 copy-start.5
  68.0 2.0 copy-start.9
  71.3 9.4 %copy-start.13 = (bf16[2048]{0:T(1024)(128)(2,1)S(1)}, bf16[2048]{0:T(1024)(128)(2,1)}, u32[]{:S(2)}) copy-start(bf16[2048]{0:T(1024)(128)(2,1)} %param.34) | copy-start | bytes 12292
  71.3 9.5 %copy-start.14 = (bf16[2048]{0:T(1024)(128)(2,1)S(1)}, bf16[2048]{0:T(1024)(128)(2,1)}, u32[]{:S(2)}) copy-start(bf16[2048]{0:T(1024)(128)(2,1)} %param.38) | copy-start | bytes 12292
  71.3 9.5 %copy-start.10 = (f32[4096,16]{0,1:T(8,128)S(1)}, f32[4096,16]{0,1:T(8,128)}, u32[]{:S(2)}) copy-start(f32[4096,16]{0,1:T(8,128)} %param.49) | copy-start | bytes 786436
  75.9 19.5 %all-to-all-start.3 = ((bf16[8,2,32768]{2,1,0:T(2,128)(2,1)}), bf16[8,2,32768]{2,1,0:T(2,128)(2,1)S(1)}, u32[]{:S(2)}, u32[]{:S(2)}) async-start(bf16[8,2,32768]{2,1,0:T(2,128)(2,1)} %reshape.228), calls=%async_computation.3 | async-start | bytes 2097152 | tf_op jit(solution)/shard_map/all_to_all | solution.py:38
  80.6 330.0 %all-gather.5.cloned.1.call-start = ((), (), s32[]{:S(2)}) async-start(), calls=%async_computation.4 | async-start | bytes 2359296 | tf_op jit(solution)/shard_map/all_gather | solution.py:89
  101.0 7.8 copy-start.3
  163.8 9.0 %copy-start.7 = (bf16[16,16,2048]{2,1,0:T(8,128)(2,1)}, bf16[16,16,2048]{2,1,0:T(8,128)(2,1)S(1)}, u32[]{:S(2)}) copy-start(bf16[16,16,2048]{2,1,0:T(8,128)(2,1)S(1)} %get-tuple-element.203) | copy-start | bytes 3145732
  163.9 13.9 %copy-start.11 = (bf16[4,4096]{1,0:T(4,128)(2,1)S(1)}, bf16[4,4096]{1,0:T(4,128)(2,1)}, u32[]{:S(2)}) copy-start(bf16[4,4096]{1,0:T(4,128)(2,1)} %param.41) | copy-start | bytes 98308
  163.9 14.0 %copy-start.12 = (bf16[4096]{0:T(1024)(128)(2,1)S(1)}, bf16[4096]{0:T(1024)(128)(2,1)}, u32[]{:S(2)}) copy-start(bf16[4096]{0:T(1024)(128)(2,1)} %param.42) | copy-start | bytes 24580
  172.8 1.3 copy-start.4
  174.5 9.4 %collective-permute-start = (bf16[3,16,4096]{2,0,1:T(4,128)(2,1)S(1)}, bf16[3,16,4096]{2,0,1:T(4,128)(2,1)S(1)}, u32[]{:S(2)}, u32[]{:S(2)}) collective-permute-start(bf16[3,16,4096]{2,0,1:T(4,128)(2,1)S(1)} %slice.44), channel_id=1, source_target_pairs={{0,1},{1,2},{2,3},{3,4},{4,5},{5,6},{6,7},{8,9},{9,10},{10,11},{11... | collective-permute-start | bytes 1179656 | tf_op jit(solution)/shard_map/ppermute | solution.py:61
  190.9 3.2 copy-start.2
  190.9 5.9 copy-start.15
  190.9 6.0 copy-start.18
  190.9 6.0 copy-start.19
  196.9 6.0 copy-start.16
  196.9 6.0 copy-start.17
  202.5 365.1 %all-gather.7.cloned.1.call-start = ((), (), s32[]{:S(2)}) async-start(), calls=%async_computation.5 | async-start | bytes 37748736 | tf_op jit(solution)/shard_map/all_gather | solution.py:88
  587.1 199.6 %copy-start.8 = (bf16[16,16,2048]{2,1,0:T(8,128)(2,1)S(1)}, bf16[16,16,2048]{2,1,0:T(8,128)(2,1)}, u32[]{:S(2)}) copy-start(bf16[16,16,2048]{2,1,0:T(8,128)(2,1)} %copy-done.7) | copy-start | bytes 3145732
  587.1 199.6 %copy-start.20 = (f32[4096]{0:T(1024)S(1)}, f32[4096]{0:T(1024)}, u32[]{:S(2)}) copy-start(f32[4096]{0:T(1024)} %param.50) | copy-start | bytes 49156
  786.7 19.8 %copy-start.1 = (bf16[2048,8,64]{0,2,1:T(8,128)(2,1)S(1)}, bf16[2048,8,64]{0,2,1:T(8,128)(2,1)}, u32[]{:S(2)}) copy-start(bf16[2048,8,64]{0,2,1:T(8,128)(2,1)} %param.31) | copy-start | bytes 6291460
Sparse Core Ops, SparseCore 0:
  202.6 25.2 all-gather.4
  410.6 156.8 all-gather.6
where the time goes:
time: 827 us; the launch traced here: 814 us
  local copies, waits for them, and re-layouts  277 us (33%)
  other arithmetic  209 us (25%)
  waiting for transfers between devices  186 us (22%)
  matrix products  101 us (12%)
  starting transfers between devices  24.8 us (3%)
  between operations  14.1 us (2%)
    dynamic_update_slice x64, local copies, waits for them, and re-layouts, mamba_mixer(): lax.scan(local_step, zero_state, (step_size, x_conv, b_mat, c_mat))  200 us
    all_gather x1, waiting for transfers between devices, mamba_mixer(): all_states = lax.all_gather(end_state, 'sp')  152 us
    reduce_sum x16, other arithmetic, carry_step(): return (ssm_state, jnp.sum(ssm_state * c_t[:, None, :], axis=-1))  83.7 us
    reduce_sum x16, other arithmetic, local_step(): return (ssm_state, jnp.sum(ssm_state * c_t[:, None, :], axis=-1))  71.5 us
    dot_general x1, matrix products, mlp_layer(): down_out = jnp.dot(act_val, w_down, preferred_element_type=jnp.float32)  29.5 us
    dot_general x1, matrix products, mamba_mixer(): jnp.einsum('tbe,ed->btd', gated_y, w_out, preferred_element_type=jnp.floa...  19.8 us
    unnamed x52, local copies, waits for them, and re-layouts  18.9 us
    reduce_sum x1, other arithmetic, mamba_mixer(): start_state = jnp.sum(carry_weight * all_states, axis=0)  17.1 us
  transfers between devices with their start and end apart: 7, of which 5 were waited for; matrix products, arithmetic and copies ran while one was open for 29% of the time, Pallas kernels for 0%

commit v1 on v0

v1 whole, which is shorter than its diff:
```python
import functools
import math

import jax
import jax.numpy as jnp
from jax import lax
from jax.experimental import pallas as pl
from jax.experimental.pallas import tpu as pltpu
from jax.sharding import PartitionSpec as P

EPS = 1e-6
CONV = 4
CH = 512
NS = 12
ST = 260
SA = 33
LOG2E = math.log2(math.e)
F32 = jnp.float32
BF16 = jnp.bfloat16


def nt_dot(a, b):
    return lax.dot_general(a, b, (((1,), (1,)), ((), ())), preferred_element_type=F32)


def nn_dot(a, b):
    return jnp.dot(a, b, preferred_element_type=F32)


def silu(v):
    return v * (1.0 / (1.0 + jnp.exp(-v)))


def softplus(v):
    return jnp.maximum(v, 0.0) + jnp.log1p(jnp.exp(-jnp.abs(v)))


def rms(v):
    return v * lax.rsqrt(jnp.mean(v * v, axis=-1, keepdims=True) + EPS)


def layer_kernel(
    hid, vecs, small, alog, wq, wk, wv, wo, wg, wu, wd, wix, wiz, wxp, wdt, wout,
    out, ring, kvw, xpw, dtw, norm, q, kv, attn, acc, act, res, xpad, conv, zg, gated, bc, dl, dc, ys, amat,
    sem, sem2,
):
    rows, dim = hid.shape
    seq = 128 if rows % 128 == 0 else rows
    n_seq = rows // seq
    inner = conv.shape[1]
    n_state = alog.shape[0]
    rank = wdt.shape[0]

    def cols(w, c, slot):
        return pltpu.make_async_copy(w.at[:, pl.ds(c * CH, CH)], ring.at[slot], sem.at[slot])

    def block(w, k, c, slot):
        return pltpu.make_async_copy(w.at[pl.ds(k * dim, dim), pl.ds(c * CH, CH)], ring.at[slot], sem.at[slot])

    def ready(slot):
        pltpu.make_async_copy(wg.at[:, pl.ds(0, CH)], ring.at[slot], sem.at[slot]).wait()

    def slot_of(p):
        return lax.rem(p + 8, NS)

    k_load = pltpu.make_async_copy(wk, kvw.at[pl.ds(0, CH)], sem2.at[0])
    v_load = pltpu.make_async_copy(wv, kvw.at[pl.ds(CH, CH)], sem2.at[1])
    xp_load = pltpu.make_async_copy(wxp, xpw, sem2.at[2])
    dt_load = pltpu.make_async_copy(wdt, dtw, sem2.at[3])
    for i in range(4):
        cols(wq, i, i).start()
    k_load.start()
    v_load.start()
    for i in range(4):
        cols(wo, i, 4 + i).start()
    cols(wg, 0, 8).start()
    cols(wu, 0, 9).start()
    cols(wg, 1, 10).start()
    cols(wu, 1, 11).start()
    xp_load.start()
    dt_load.start()

    def normalize(src, gain_row):
        gain = vecs[gain_row:gain_row + 1, :]

        def body(i, _):
            r = pl.ds(pl.multiple_of(i * 16, 16), 16)
            norm[r, :] = (rms(src[r, :].astype(F32)) * gain).astype(BF16)
            return 0

        lax.fori_loop(0, rows // 16, body, 0, unroll=2)

    for j in range(inner // 128):
        a = -jnp.exp(alog[:, j * 128:(j + 1) * 128]) * LOG2E
        amat[pl.ds(j, n_state, stride=SA), :] = a

    normalize(hid, 0)
    for i in range(4):
        ready(i)
        term = nt_dot(norm[:, i * CH:(i + 1) * CH], ring[i])
        if i == 0:
            acc[...] = term
        elif i < 3:
            acc[...] += term
        else:
            q[...] = (acc[...] + term).astype(BF16)
        if i % 2 == 0:
            cols(wg, 2 + i // 2, i).start()
        else:
            cols(wu, 2 + i // 2, i).start()
    k_load.wait()
    v_load.wait()
    kv[...] = nt_dot(norm[...], kvw[...]).astype(BF16)

    head = 64
    lane = lax.broadcasted_iota(jnp.int32, (seq, 128), 1)
    low = lane < head
    causal = (lax.rem(lax.broadcasted_iota(jnp.int32, (2 * seq, 128), 0), seq)
              >= lax.broadcasted_iota(jnp.int32, (2 * seq, 128), 1))
    pairs = CH // 128

    def spread(tile, upper):
        if upper:
            hi = jnp.where(low, 0.0, tile)
            lo = pltpu.roll(hi, head, 1)
        else:
            lo = jnp.where(low, tile, 0.0)
            hi = pltpu.roll(lo, head, 1)
        return jnp.concatenate([lo, hi], axis=0).astype(BF16)

    def attend(it, _):
        b = lax.div(it, pairs)
        m = lax.rem(it, pairs)
        r = pl.ds(pl.multiple_of(b * seq, seq), seq)
        kt = kv[r, pl.ds(pl.multiple_of(m * 128, 128), 128)].astype(F32)
        vt = kv[r, pl.ds(pl.multiple_of(CH + m * 128, 128), 128)].astype(F32)
        for par in range(2):
            k2 = spread(kt, par)
            v2 = spread(vt, par)
            c0 = pl.multiple_of((2 * m + par) * 256, 128)
            qs = jnp.concatenate([q[r, pl.ds(c0, 128)], q[r, pl.ds(c0 + 128, 128)]], axis=0)
            s = nt_dot(qs, k2)
            ps = []
            for h in range(2):
                sh = jnp.where(causal, s[:, h * 128:(h + 1) * 128] * head ** -0.5, -jnp.inf)
                e = jnp.exp(sh - jnp.max(sh, axis=-1, keepdims=True))
                ps.append((e * (1.0 / jnp.sum(e, axis=-1, keepdims=True))).astype(BF16))
            o = nn_dot(jnp.concatenate(ps, axis=1), v2).astype(BF16)
            attn[r, pl.ds(c0, 128)] = o[:seq]
            attn[r, pl.ds(c0 + 128, 128)] = o[seq:]
        return 0

    lax.fori_loop(0, n_seq * pairs, attend, 0)

    def out_proj(n, _):
        ready(4 + n)
        c = pl.ds(pl.multiple_of(n * CH, CH), CH)
        res[:, c] = (hid[:, c].astype(F32) + nn_dot(attn[...], ring[4 + n])).astype(BF16)
        block(wd, 0, n, 4 + n).start()
        return 0

    lax.fori_loop(0, 4, out_proj, 0)

    normalize(res, 1)

    def mlp(s, _):
        def up(n, _):
            sg = slot_of(2 * n)
            su = slot_of(2 * n + 1)
            ready(sg)
            ready(su)
            gate = nn_dot(norm[...], ring[sg])
            upv = nn_dot(norm[...], ring[su])
            act[:, pl.ds(pl.multiple_of(n * CH, CH), CH)] = (silu(gate) * upv).astype(BF16)

            @pl.when(s < 3)
            def _():
                cols(wg, 4 * (s + 1) + n, sg).start()
                cols(wu, 4 * (s + 1) + n, su).start()

            @pl.when(s == 3)
            def _():
                cols(wix, 2 * n, sg).start()
                cols(wix, 2 * n + 1, su).start()

            return 0

        lax.fori_loop(0, 4, up, 0)

        def down(n, _):
            sd = slot_of(8 + n)
            ready(sd)
            c = pl.ds(pl.multiple_of(n * CH, CH), CH)
            term = nn_dot(act[...], ring[sd])

            @pl.when(s == 0)
            def _():
                acc[:, c] = res[:, c].astype(F32) + term

            @pl.when((s > 0) & (s < 3))
            def _():
                acc[:, c] += term

            @pl.when(s == 3)
            def _():
                res[:, c] = (acc[:, c] + term).astype(BF16)

            @pl.when(s < 3)
            def _():
                block(wd, s + 1, n, sd).start()

            @pl.when(s == 3)
            def _():
                cols(wiz, n, sd).start()

            return 0

        lax.fori_loop(0, 4, down, 0)
        return 0

    lax.fori_loop(0, 4, mlp, 0)

    normalize(res, 2)
    pitch = seq + 8
    for b in range(n_seq):
        xpad[pl.ds(b * pitch, 8), :] = jnp.zeros((8, CH), F32)

    def inx(e, _):
        sl = slot_of(e)
        ready(sl)
        xi = nn_dot(norm[...], ring[sl]).astype(BF16).astype(F32)

        @pl.when(e < 4)
        def _():
            cols(wiz, 4 + e, sl).start()

        @pl.when(e >= 4)
        def _():
            block(wout, lax.rem(e, 2), lax.div(e - 4, 2), sl).start()

        half = lax.div(e, 4)
        c_in = pl.ds(pl.multiple_of(lax.rem(e, 4) * CH, CH), CH)
        bias = vecs[pl.ds(3 + half, 1), c_in]
        taps = [vecs[pl.ds(9 + 2 * j + half, 1), c_in] for j in range(CONV)]
        c = pl.ds(pl.multiple_of(e * CH, CH), CH)
        for b in range(n_seq):
            xpad[pl.ds(b * pitch + 8, seq), :] = xi[b * seq:(b + 1) * seq]
        for b in range(n_seq):
            v = bias
            for j in range(CONV):
                v = v + xpad[pl.ds(b * pitch + 8 - (CONV - 1) + j, seq), :] * taps[j]
            conv[pl.ds(b * seq, seq), c] = silu(v).astype(BF16)
        return 0

    lax.fori_loop(0, 8, inx, 0)

    xp_load.wait()
    dt_load.wait()
    r = nt_dot(conv[...], xpw[...])
    dt_in = (rms(r[:, :rank]) * small[:, :rank]).astype(BF16)
    bm = rms(r[:, rank:rank + n_state]) * small[:, rank:rank + n_state]
    cm = rms(r[:, rank + n_state:rank + 2 * n_state]) * small[:, rank + n_state:rank + 2 * n_state]
    for n in range(n_state):
        bc[n] = jnp.broadcast_to(bm[:, n:n + 1], (rows, 128))
        bc[n_state + n] = jnp.broadcast_to(cm[:, n:n + 1], (rows, 128))

    def inz(e, _):
        sl = slot_of(8 + e)
        ready(sl)
        zg[:, pl.ds(pl.multiple_of(e * CH, CH), CH)] = nn_dot(norm[...], ring[sl]).astype(BF16)

        @pl.when(e < 4)
        def _():
            block(wout, lax.rem(e, 2), 2 + lax.div(e, 2), sl).start()

        return 0

    lax.fori_loop(0, 8, inz, 0)

    for blk in range(inner // 1024):
        for j in range(8):
            c0 = blk * 1024 + j * 128
            pre = nn_dot(dt_in, dtw[:, c0:c0 + 128]) + vecs[5 + c0 // 2048:6 + c0 // 2048, c0 % 2048:c0 % 2048 + 128]
            step = softplus(pre)
            dl[pl.ds(j * ST, rows), :] = step
            dc[pl.ds(j * ST, rows), :] = step * conv[:, c0:c0 + 128].astype(F32)
        a_rows = [amat[pl.ds(n * SA + blk * 8, 8), :] for n in range(n_state)]

        def one_seq(b, _):
            def step_fn(t, hs):
                row = b * seq + t
                d = dl[pl.ds(row, 8, stride=ST), :]
                x = dc[pl.ds(row, 8, stride=ST), :]
                new = []
                y = None
                for n in range(n_state):
                    bv = jnp.broadcast_to(bc[n, pl.ds(row, 1), :], (8, 128))
                    cv = jnp.broadcast_to(bc[n_state + n, pl.ds(row, 1), :], (8, 128))
                    hn = jnp.exp2(d * a_rows[n]) * hs[n] + x * bv
                    new.append(hn)
                    y = hn * cv if y is None else y + hn * cv
                ys[pl.ds(row, 8, stride=ST), :] = y
                return tuple(new)

            lax.fori_loop(0, seq, step_fn, tuple(jnp.zeros((8, 128), F32) for _ in range(n_state)), unroll=4)
            return 0

        lax.fori_loop(0, n_seq, one_seq, 0)
        for j in range(8):
            c0 = blk * 1024 + j * 128
            skip = vecs[7 + c0 // 2048:8 + c0 // 2048, c0 % 2048:c0 % 2048 + 128]
            y = ys[pl.ds(j * ST, rows), :] + skip * conv[:, c0:c0 + 128].astype(F32)
            gated[:, c0:c0 + 128] = (y * silu(zg[:, c0:c0 + 128].astype(F32))).astype(BF16)

    def final(n, _):
        s0 = slot_of(4 + 2 * n)
        s1 = slot_of(5 + 2 * n)
        ready(s0)
        ready(s1)
        c = pl.ds(pl.multiple_of(n * CH, CH), CH)
        y = nn_dot(gated[:, :dim], ring[s0]) + nn_dot(gated[:, dim:], ring[s1])
        out[:, c] = (res[:, c].astype(F32) + y).astype(BF16)
        return 0

    lax.fori_loop(0, 4, final, 0)


def local_layers(hid, attn_norm, w_q, w_k, w_v, w_o, mlp_norm, w_gate, w_up, w_down, mamba_norm, w_in_x, w_in_z,
                 conv_w, conv_b, w_xproj, dt_norm, b_norm, c_norm, w_dt, dt_bias, a_log, d_skip, w_out):
    rows, dim = hid.shape
    inner, n_state = a_log.shape
    rank = w_dt.shape[0]
    flat = [v.astype(F32).reshape(-1) for v in (attn_norm, mlp_norm, mamba_norm, conv_b, dt_bias, d_skip, conv_w)]
    vecs = jnp.concatenate(flat).reshape(-1, dim)
    small = jnp.concatenate([dt_norm, b_norm, c_norm]).reshape(1, -1)
    wq_t = w_q.transpose(1, 2, 0).reshape(-1, dim)
    wk_t = w_k.transpose(1, 2, 0).reshape(-1, dim)
    wv_t = w_v.transpose(1, 2, 0).reshape(-1, dim)
    kv_dim = wk_t.shape[0]
    wo = w_o.reshape(-1, dim)
    wxp = w_xproj.T
    vm = pl.BlockSpec(memory_space=pltpu.VMEM)
    hbm = pl.BlockSpec(memory_space=pl.ANY)
    return pl.pallas_call(
        layer_kernel,
        out_shape=jax.ShapeDtypeStruct((rows, dim), BF16),
        in_specs=[vm] * 4 + [hbm] * 12,
        out_specs=vm,
        scratch_shapes=[
            pltpu.VMEM((NS, dim, CH), BF16),
            pltpu.VMEM((2 * kv_dim, dim), BF16),
            pltpu.VMEM(wxp.shape, BF16),
            pltpu.VMEM(w_dt.shape, BF16),
            pltpu.VMEM((rows, dim), BF16),
            pltpu.VMEM((rows, dim), BF16),
            pltpu.VMEM((rows, 2 * kv_dim), BF16),
            pltpu.VMEM((rows, dim), BF16),
            pltpu.VMEM((rows, dim), F32),
            pltpu.VMEM((rows, dim), BF16),
            pltpu.VMEM((rows, dim), BF16),
            pltpu.VMEM((rows + 8 * (rows // 128), CH), F32),
            pltpu.VMEM((rows, inner), BF16),
            pltpu.VMEM((rows, inner), BF16),
            pltpu.VMEM((rows, inner), BF16),
            pltpu.VMEM((2 * n_state, rows, 128), F32),
            pltpu.VMEM((8 * ST, 128), F32),
            pltpu.VMEM((8 * ST, 128), F32),
            pltpu.VMEM((8 * ST, 128), F32),
            pltpu.VMEM((n_state * SA, 128), F32),
            pltpu.SemaphoreType.DMA((NS,)),
            pltpu.SemaphoreType.DMA((4,)),
        ],
        compiler_params=pltpu.CompilerParams(vmem_limit_bytes=63 * 1024 * 1024),
        cost_estimate=pl.CostEstimate(flops=45_000_000_000, bytes_accessed=180_000_000, transcendentals=20_000_000),
        name="layers",
    )(hid, vecs, small, a_log.T, wq_t, wk_t, wv_t, wo, w_gate, w_up, w_down, w_in_x, w_in_z, wxp, w_dt, w_out)


def group_layers(hidden, *weights, n_shards):
    n_batch, tok, dim = hidden.shape
    per = n_batch // n_shards
    seq = lax.all_to_all(hidden.reshape(n_shards, per, tok, dim), "sp", 0, 0)
    seq = seq.transpose(1, 0, 2, 3).reshape(per * n_shards * tok, dim)
    done = local_layers(seq, *weights)
    done = done.reshape(per, n_shards, tok, dim).transpose(1, 0, 2, 3)
    return lax.all_to_all(done, "sp", 0, 0).reshape(n_batch, tok, dim)


def solution(mesh):
    act_spec = P("dp", "sp", None)
    return jax.shard_map(
        functools.partial(group_layers, n_shards=mesh.shape["sp"]),
        mesh=mesh,
        in_specs=(act_spec,) + (P(),) * 23,
        out_specs=act_spec,
        check_vma=False,
    )
```

time: 827 us -> 148 us (0.18); the launches traced: 814 us -> 147 us
  local copies, waits for them, and re-layouts: 277 us -> 5.46 us
  other arithmetic: 209 us -> 4.88 us
  waiting for transfers between devices: 186 us -> 7.7 us
  Pallas kernels: 0 us -> 104 us
  matrix products: 101 us -> 0 us
  starting transfers between devices: 24.8 us -> 6.01 us
  blocking collectives: 0 us -> 18.6 us
  between operations: 14.1 us -> 0.03 us
    dynamic_update_slice x64 -> x0, local copies, waits for them, and re-layouts: 200 us -> none  [mamba_mixer(): lax.scan(local_step, zero_state, (step_size, x_conv, b_mat, c_mat))]
    reduce_sum x39 -> x0, other arithmetic: 179 us -> none  [the longest x16 83.7 us: carry_step(): return (ssm_state, jnp.sum(ssm_state * c_t[:, None, :], axis=-1))]
    all_gather x2 -> x0, waiting for transfers between devices: 152 us -> none  [the longest x1 152 us: mamba_mixer(): all_states = lax.all_gather(end_state, 'sp')]
    pallas_call x0 -> x1, Pallas kernels: none -> 104 us  [local_layers(): pl.pallas_call(layer_kernel, out_shape=jax.ShapeDtypeStruct((rows, dim),...]
    dot_general x12 -> x0, matrix products: 101 us -> none  [the longest x1 29.5 us: mlp_layer(): down_out = jnp.dot(act_val, w_down, preferred_element_type=jnp.float32)]
    mul x64 -> x0, local copies, waits for them, and re-layouts: 31.5 us -> none  [the longest x16 15.6 us: local_step(): decay_t = jnp.exp(step_t[:, :, None] * a_mat)]
    all_to_all x4 -> x1, waiting for transfers between devices: 28.2 us -> 7.7 us  [group_layers(): seq = lax.all_to_all(hidden.reshape(n_shards, per, tok, dim), 'sp', 0, 0)]
    all_to_all x0 -> x1, blocking collectives: none -> 18.6 us  [group_layers(): return lax.all_to_all(done, 'sp', 0, 0).reshape(n_batch, tok, dim)]
  transfers between devices with their start and end apart: 7 -> 1, of which waited for: 5 -> 1; matrix products, arithmetic and copies ran while one was open for 29% -> 5% of each run, Pallas kernels for 0% -> 0%
where the time goes in v1:
time: 148 us; the launch traced here: 147 us
  Pallas kernels  104 us (70%)
  blocking collectives  18.6 us (13%)
  waiting for transfers between devices  7.7 us (5%)
  starting transfers between devices  6.01 us (4%)
  local copies, waits for them, and re-layouts  5.46 us (4%)
  other arithmetic  4.88 us (3%)
    pallas_call x1, Pallas kernels, local_layers(): pl.pallas_call(layer_kernel, out_shape=jax.ShapeDtypeStruct((rows, dim),...  104 us
    all_to_all x1, blocking collectives, group_layers(): return lax.all_to_all(done, 'sp', 0, 0).reshape(n_batch, tok, dim)  18.6 us
    all_to_all x1, waiting for transfers between devices, group_layers(): seq = lax.all_to_all(hidden.reshape(n_shards, per, tok, dim), 'sp', 0, 0)  7.7 us
    all_to_all x1, starting transfers between devices, group_layers(): seq = lax.all_to_all(hidden.reshape(n_shards, per, tok, dim), 'sp', 0, 0)  6.01 us
    unnamed x5, other arithmetic  3.53 us
  transfers between devices with their start and end apart: 1, of which 1 were waited for; matrix products, arithmetic and copies ran while one was open for 5% of the time, Pallas kernels for 0%

profile of v1, /device:TPU:81, one launch (start us, length us, event | category | flops | bytes accessed | tf_op | source)
XLA Modules:
  0.0 147.1 jit_solution(8660587674678651189)
XLA Ops:
  0.0 6.0 %all-to-all-start = ((bf16[8,2,16,2048]{3,2,1,0:T(8,128)(2,1)}), bf16[8,2,16,2048]{3,2,1,0:T(8,128)(2,1)S(1)}, u32[]{:S(2)}, u32[]{:S(2)}) async-start(bf16[8,2,16,2048]{3,2,1,0:T(8,128)(2,1)} %bitcast.34), calls=%async_computation | async-start | bytes 2097152 | tf_op jit(solution)/shard_map/all_to_all | solution.py:382
  6.0 0.8 convert_bitcast_fusion
  6.8 0.7 convert_dynamic-update-slice_fusion.3
  7.5 0.7 convert_dynamic-update-slice_fusion.2
  8.2 0.7 convert_dynamic-update-slice_fusion.1
  8.9 0.7 convert_dynamic-update-slice_fusion
  9.6 0.7 constant_dynamic-update-slice_fusion.2
  10.3 0.7 constant_dynamic-update-slice_fusion.1
  11.0 0.7 reshape.40.vecs
  11.7 1.4 pad_maximum_fusion
  13.1 7.7 %all-to-all-done = bf16[8,2,16,2048]{3,2,1,0:T(8,128)(2,1)S(1)} async-done(((bf16[8,2,16,2048]{3,2,1,0:T(8,128)(2,1)}), bf16[8,2,16,2048]{3,2,1,0:T(8,128)(2,1)S(1)}, u32[]{:S(2)}, u32[]{:S(2)}) %all-to-all-start) | async-done | bytes 1048608 | tf_op jit(solution)/shard_map/all_to_all | solution.py:382
  20.8 1.0 copy.27
  21.8 104.4 %layers.1 = bf16[256,2048]{1,0:T(8,128)(2,1)} custom-call(bf16[256,2048]{1,0:T(8,128)(2,1)} %bitcast.26, f32[17,2048]{1,0:T(8,128)} %reshape.40.vecs, f32[1,160]{1,0:T(1,128)} %bitcast.37, f32[16,4096]{1,0:T(8,128)} %bitcast.35, bf16[2048,2048]{1,0:T(8,128)(2,1)} %bitcast.24, bf16[512,2048]{1,0:T(8,128)(2,1)} %bitcast.31, bf16[512,2048]{1,0:T(8,128)(2,1)} %bitcast.32, ...), custom_call_target="tpu_custom_call" | custom-call | flops 44999999488 | bytes 180000000 | tf_op jit(solution)/shard_map/layers/pallas_call | solution.py:344
  126.2 1.3 copy.31
  127.5 18.6 %all_to_all.10 = bf16[8,2,16,2048]{3,2,1,0:T(8,128)(2,1)S(1)} all-to-all(bf16[8,2,16,2048]{3,2,1,0:T(8,128)(2,1)S(1)} %bitcast.29), channel_id=1, replica_groups=mesh['dp'=4,'sp'=8] {'sp'}, dimensions={0} | all-to-all | bytes 2097152 | tf_op jit(solution)/shard_map/all_to_all | solution.py:386
  146.2 1.0 copy.39
  (2 shorter events, 0.0 us)
Async XLA Ops:
  0.0 20.8 %all-to-all-start = ((bf16[8,2,16,2048]{3,2,1,0:T(8,128)(2,1)}), bf16[8,2,16,2048]{3,2,1,0:T(8,128)(2,1)S(1)}, u32[]{:S(2)}, u32[]{:S(2)}) async-start(bf16[8,2,16,2048]{3,2,1,0:T(8,128)(2,1)} %bitcast.34), calls=%async_computation | async-start | bytes 2097152 | tf_op jit(solution)/shard_map/all_to_all | solution.py:382

commit v2 on v1

v2 whole, which is shorter than its diff:
```python
import functools
import math

import jax
import jax.numpy as jnp
from jax import lax
from jax.experimental import pallas as pl
from jax.experimental.pallas import tpu as pltpu
from jax.sharding import PartitionSpec as P

EPS = 1e-6
CONV = 4
CH = 512
NS = 12
ST = 260
SA = 33
LOG2E = math.log2(math.e)
F32 = jnp.float32
BF16 = jnp.bfloat16


def nt_dot(a, b):
    return lax.dot_general(a, b, (((1,), (1,)), ((), ())), preferred_element_type=F32)


def nn_dot(a, b):
    return jnp.dot(a, b, preferred_element_type=F32)


def silu(v):
    return v * (1.0 / (1.0 + jnp.exp(-v)))


def softplus(v):
    return jnp.maximum(v, 0.0) + jnp.log1p(jnp.exp(-jnp.abs(v)))


def rms(v):
    return v * lax.rsqrt(jnp.mean(v * v, axis=-1, keepdims=True) + EPS)


def layer_kernel(
    n_dev, axis, x_in, attn_norm, mlp_norm, mamba_norm, conv_w, conv_b, dt_norm, b_norm, c_norm, dt_bias, d_skip, alog,
    wq, wk, wv, wo, wg, wu, wd, wix, wiz, wxp, wdt, wout,
    out, ring, kvw, xpw, dtw, hid, norm, q, kv, acc, res, xpad, conv, zg, bc, dl, dc, ys, amat,
    sem, sem2, in_send, in_recv, out_send, out_recv, own_sem,
):
    n_batch, tok, dim = x_in.shape
    per = n_batch // n_dev
    seq = tok * n_dev
    rows = per * seq
    inner = conv.shape[1]
    n_state = alog.shape[0]
    rank = wdt.shape[0]
    me = lax.axis_index(axis) if n_dev > 1 else 0
    act = q

    def peer_of(k):
        chips = n_dev // 2
        chip = lax.rem(lax.div(me, 2) + k // 2, chips)
        return chip * 2 + lax.rem(lax.rem(me, 2) + k % 2, 2)

    order = sorted(range(1, n_dev), key=lambda k: (-min(k // 2, n_dev // 2 - k // 2), k % 2, k))

    def cols(w, c, slot):
        return pltpu.make_async_copy(w.at[:, pl.ds(c * CH, CH)], ring.at[slot], sem.at[slot])

    def block(w, k, c, slot):
        return pltpu.make_async_copy(w.at[pl.ds(k * dim, dim), pl.ds(c * CH, CH)], ring.at[slot], sem.at[slot])

    def ready(slot):
        pltpu.make_async_copy(wg.at[:, pl.ds(0, CH)], ring.at[slot], sem.at[slot]).wait()

    def slot_of(p):
        return lax.rem(p + 8, NS)

    def send_in(k, b):
        to = peer_of(k)
        return pltpu.make_async_remote_copy(
            src_ref=x_in.at[to * per + b],
            dst_ref=hid.at[pl.ds(pl.multiple_of(b * seq + me * tok, tok), tok)],
            send_sem=in_send.at[k - 1, b],
            recv_sem=in_recv.at[k - 1, b],
            device_id={axis: to},
            device_id_type=pl.DeviceIdType.MESH,
        )

    own_in = [
        pltpu.make_async_copy(
            x_in.at[me * per + b],
            hid.at[pl.ds(pl.multiple_of(b * seq + me * tok, tok), tok)],
            own_sem.at[b, dim // CH],
        )
        for b in range(per)
    ]

    k_load = pltpu.make_async_copy(wk, kvw.at[pl.ds(0, CH)], sem2.at[0])
    v_load = pltpu.make_async_copy(wv, kvw.at[pl.ds(CH, CH)], sem2.at[1])
    xp_load = pltpu.make_async_copy(wxp, xpw, sem2.at[2])
    dt_load = pltpu.make_async_copy(wdt, dtw, sem2.at[3])
    for copy in own_in:
        copy.start()
    if n_dev > 1:
        barrier = pltpu.get_barrier_semaphore()
        for k in range(1, n_dev):
            pl.semaphore_signal(barrier, inc=1, device_id={axis: peer_of(k)}, device_id_type=pl.DeviceIdType.MESH)
    for i in range(4):
        cols(wq, i, i).start()
    k_load.start()
    v_load.start()
    if n_dev > 1:
        pl.semaphore_wait(barrier, n_dev - 1)
        for b in range(per):
            for k in order:
                send_in(k, b).start()
    for i in range(4):
        cols(wo, i, 4 + i).start()
    cols(wg, 0, 8).start()
    cols(wu, 0, 9).start()
    cols(wg, 1, 10).start()
    cols(wu, 1, 11).start()
    xp_load.start()
    dt_load.start()

    def normalize(src, gain_ref, start=0, count=rows):
        gain = gain_ref[...].astype(F32).reshape(1, dim)

        def body(i, _):
            r = pl.ds(pl.multiple_of(start + i * 16, 16), 16)
            norm[r, :] = (rms(src[r, :].astype(F32)) * gain).astype(BF16)
            return 0

        lax.fori_loop(0, count // 16, body, 0, unroll=2)

    for j in range(inner // 128):
        a = -jnp.exp(alog[:, j * 128:(j + 1) * 128]) * LOG2E
        amat[pl.ds(j, n_state, stride=SA), :] = a

    head = 64
    lane = lax.broadcasted_iota(jnp.int32, (seq, 128), 1)
    low = lane < head
    causal = (lax.rem(lax.broadcasted_iota(jnp.int32, (2 * seq, 128), 0), seq)
              >= lax.broadcasted_iota(jnp.int32, (2 * seq, 128), 1))
    pairs = CH // 128

    def spread(tile, upper):
        if upper:
            hi = jnp.where(low, 0.0, tile)
            lo = pltpu.roll(hi, head, 1)
        else:
            lo = jnp.where(low, tile, 0.0)
            hi = pltpu.roll(lo, head, 1)
        return jnp.concatenate([lo, hi], axis=0).astype(BF16)

    for b in range(per):
        own_in[b].wait()
        if n_dev > 1:
            for k in order:
                send_in(k, b).wait_recv()
        rb = pl.ds(b * seq, seq)
        normalize(hid, attn_norm, b * seq, seq)
        for i in range(4):
            if b == 0:
                ready(i)
            term = nt_dot(norm[rb, i * CH:(i + 1) * CH], ring[i])
            if i == 0:
                acc[rb, :] = term
            elif i < 3:
                acc[rb, :] += term
            else:
                q[rb, :] = (acc[rb, :] + term).astype(BF16)
            if b == per - 1:
                if i % 2 == 0:
                    cols(wg, 2 + i // 2, i).start()
                else:
                    cols(wu, 2 + i // 2, i).start()
        if b == 0:
            k_load.wait()
            v_load.wait()
        kv[rb, :] = nt_dot(norm[rb, :], kvw[...]).astype(BF16)

        def attend(m, _, rb=rb):
            kt = kv[rb, pl.ds(pl.multiple_of(m * 128, 128), 128)].astype(F32)
            vt = kv[rb, pl.ds(pl.multiple_of(CH + m * 128, 128), 128)].astype(F32)
            for par in range(2):
                k2 = spread(kt, par)
                v2 = spread(vt, par)
                c0 = pl.multiple_of((2 * m + par) * 256, 128)
                qs = jnp.concatenate([q[rb, pl.ds(c0, 128)], q[rb, pl.ds(c0 + 128, 128)]], axis=0)
                s = nt_dot(qs, k2)
                ps = []
                for h in range(2):
                    sh = jnp.where(causal, s[:, h * 128:(h + 1) * 128] * head ** -0.5, -jnp.inf)
                    e = jnp.exp(sh - jnp.max(sh, axis=-1, keepdims=True))
                    ps.append((e * (1.0 / jnp.sum(e, axis=-1, keepdims=True))).astype(BF16))
                o = nn_dot(jnp.concatenate(ps, axis=1), v2).astype(BF16)
                norm[rb, pl.ds(c0, 128)] = o[:seq]
                norm[rb, pl.ds(c0 + 128, 128)] = o[seq:]
            return 0

        lax.fori_loop(0, pairs, attend, 0)

    def out_proj(n, _):
        ready(4 + n)
        c = pl.ds(pl.multiple_of(n * CH, CH), CH)
        res[:, c] = (hid[:, c].astype(F32) + nn_dot(norm[...], ring[4 + n])).astype(BF16)
        block(wd, 0, n, 4 + n).start()
        return 0

    lax.fori_loop(0, 4, out_proj, 0)

    normalize(res, mlp_norm)

    def mlp(s, _):
        def up(n, _):
            sg = slot_of(2 * n)
            su = slot_of(2 * n + 1)
            ready(sg)
            ready(su)
            gate = nn_dot(norm[...], ring[sg])
            upv = nn_dot(norm[...], ring[su])
            act[:, pl.ds(pl.multiple_of(n * CH, CH), CH)] = (silu(gate) * upv).astype(BF16)

            @pl.when(s < 3)
            def _():
                cols(wg, 4 * (s + 1) + n, sg).start()
                cols(wu, 4 * (s + 1) + n, su).start()

            @pl.when(s == 3)
            def _():
                cols(wix, 2 * n, sg).start()
                cols(wix, 2 * n + 1, su).start()

            return 0

        lax.fori_loop(0, 4, up, 0)

        def down(n, _):
            sd = slot_of(8 + n)
            ready(sd)
            c = pl.ds(pl.multiple_of(n * CH, CH), CH)
            term = nn_dot(act[...], ring[sd])

            @pl.when(s == 0)
            def _():
                acc[:, c] = res[:, c].astype(F32) + term

            @pl.when((s > 0) & (s < 3))
            def _():
                acc[:, c] += term

            @pl.when(s == 3)
            def _():
                res[:, c] = (acc[:, c] + term).astype(BF16)

            @pl.when(s < 3)
            def _():
                block(wd, s + 1, n, sd).start()

            @pl.when(s == 3)
            def _():
                cols(wiz, n, sd).start()

            return 0

        lax.fori_loop(0, 4, down, 0)
        return 0

    lax.fori_loop(0, 4, mlp, 0)

    normalize(res, mamba_norm)
    pitch = seq + 8
    for i in range(2):
        for b in range(per):
            xpad[i, pl.ds(b * pitch, 8), :] = jnp.zeros((8, CH), F32)

    def conv_chunk(e):
        i = lax.rem(e, 2)
        c = pl.ds(pl.multiple_of(e * CH, CH), CH)
        bias = conv_b[c].astype(F32).reshape(1, CH)
        taps = [conv_w[j:j + 1, c].astype(F32) for j in range(CONV)]
        for b in range(per):
            v = bias
            for j in range(CONV):
                v = v + xpad[i, pl.ds(b * pitch + 8 - (CONV - 1) + j, seq), :] * taps[j]
            conv[pl.ds(b * seq, seq), c] = silu(v).astype(BF16)

    def inx(e, _):
        sl = slot_of(e)
        ready(sl)
        conv_chunk(jnp.maximum(e - 1, 0))
        xi = nn_dot(norm[...], ring[sl]).astype(BF16).astype(F32)
        for b in range(per):
            xpad[lax.rem(e, 2), pl.ds(b * pitch + 8, seq), :] = xi[b * seq:(b + 1) * seq]

        @pl.when(e < 4)
        def _():
            cols(wiz, 4 + e, sl).start()

        @pl.when(e >= 4)
        def _():
            block(wout, lax.rem(e, 2), lax.div(e - 4, 2), sl).start()

        return 0

    lax.fori_loop(0, inner // CH, inx, 0)
    conv_chunk(jnp.int32(inner // CH - 1))

    xp_load.wait()
    dt_load.wait()
    r = nt_dot(conv[...], xpw[...])
    dt_in = (rms(r[:, :rank]) * dt_norm[...].reshape(1, rank)).astype(BF16)
    bm = rms(r[:, rank:rank + n_state]) * b_norm[...].reshape(1, n_state)
    cm = rms(r[:, rank + n_state:rank + 2 * n_state]) * c_norm[...].reshape(1, n_state)
    for n in range(n_state):
        bc[n] = jnp.broadcast_to(bm[:, n:n + 1], (rows, 128))
        bc[n_state + n] = jnp.broadcast_to(cm[:, n:n + 1], (rows, 128))
    kv[:, :rank] = dt_in

    def inz(e, _):
        sl = slot_of(8 + e)
        ready(sl)
        c = pl.ds(pl.multiple_of(e * CH, CH), CH)
        step = softplus(nn_dot(kv[:, :rank], dtw[:, c]) + dt_bias[c].reshape(1, CH))
        prod = step * conv[:, c].astype(F32)
        for j in range(CH // 128):
            at = pl.ds((e * (CH // 128) + j) * ST, rows)
            dl[at, :] = step[:, j * 128:(j + 1) * 128]
            dc[at, :] = prod[:, j * 128:(j + 1) * 128]
        zg[:, c] = nn_dot(norm[...], ring[sl]).astype(BF16)

        @pl.when(e < 4)
        def _():
            block(wout, lax.rem(e, 2), 2 + lax.div(e, 2), sl).start()

        return 0

    lax.fori_loop(0, inner // CH, inz, 0)

    def send_out(k, b, n):
        to = peer_of(k)
        return pltpu.make_async_remote_copy(
            src_ref=q.at[pl.ds(pl.multiple_of(b * seq + to * tok, tok), tok), pl.ds(n * CH, CH)],
            dst_ref=out.at[me * per + b, :, pl.ds(n * CH, CH)],
            send_sem=out_send,
            recv_sem=out_recv,
            device_id={axis: to},
            device_id_type=pl.DeviceIdType.MESH,
        )

    def own_out(b, n):
        return pltpu.make_async_copy(
            q.at[pl.ds(pl.multiple_of(b * seq + me * tok, tok), tok), pl.ds(n * CH, CH)],
            out.at[me * per + b, :, pl.ds(n * CH, CH)],
            own_sem.at[b, n],
        )

    for b in range(per):
        rb = pl.ds(b * seq, seq)

        def scan_block(blk, _, b=b, rb=rb):
            base = blk * (8 * ST) + b * seq
            a_rows = [amat[pl.ds(n * SA + blk * 8, 8), :] for n in range(n_state)]

            def step_fn(t, hs):
                at = pl.ds(base + t, 8, stride=ST)
                d = dl[at, :]
                x = dc[at, :]
                new = []
                y = None
                for n in range(n_state):
                    bv = jnp.broadcast_to(bc[n, pl.ds(b * seq + t, 1), :], (8, 128))
                    cv = jnp.broadcast_to(bc[n_state + n, pl.ds(b * seq + t, 1), :], (8, 128))
                    hn = jnp.exp2(d * a_rows[n]) * hs[n] + x * bv
                    new.append(hn)
                    y = hn * cv if y is None else y + hn * cv
                ys[pl.ds(t, 8, stride=seq + 4), :] = y
                return tuple(new)

            lax.fori_loop(0, seq, step_fn, tuple(jnp.zeros((8, 128), F32) for _ in range(n_state)), unroll=4)
            for j in range(8):
                c = pl.ds(pl.multiple_of(blk * 1024 + j * 128, 128), 128)
                y = ys[pl.ds(j * (seq + 4), seq), :] + d_skip[c].reshape(1, 128) * conv[rb, c].astype(F32)
                zg[rb, c] = (y * silu(zg[rb, c].astype(F32))).astype(BF16)
            return 0

        lax.fori_loop(0, inner // 1024, scan_block, 0)

        for n in range(dim // CH):
            s0 = (4 + 2 * n + 8) % NS
            s1 = (5 + 2 * n + 8) % NS
            if b == 0:
                ready(s0)
                ready(s1)
            c = slice(n * CH, (n + 1) * CH)
            y = nn_dot(zg[rb, :dim], ring[s0]) + nn_dot(zg[rb, dim:], ring[s1])
            q[rb, c] = (res[rb, c].astype(F32) + y).astype(BF16)
            own_out(b, n).start()
            if n_dev > 1:
                for k in order:
                    send_out(k, b, n).start()

    for b in range(per):
        for n in range(dim // CH):
            own_out(b, n).wait()
    if n_dev > 1:
        for b in range(per):
            for k in order:
                send_in(k, b).wait_send()
        everything = pltpu.make_async_remote_copy(
            src_ref=out.at[pl.ds(0, n_batch - per)],
            dst_ref=out.at[pl.ds(0, n_batch - per)],
            send_sem=out_send,
            recv_sem=out_recv,
            device_id={axis: peer_of(1)},
            device_id_type=pl.DeviceIdType.MESH,
        )
        everything.wait_send()
        everything.wait_recv()


def local_layers(n_dev, axis, hidden, attn_norm, w_q, w_k, w_v, w_o, mlp_norm, w_gate, w_up, w_down, mamba_norm,
                 w_in_x, w_in_z, conv_w, conv_b, w_xproj, dt_norm, b_norm, c_norm, w_dt, dt_bias, a_log, d_skip, w_out):
    n_batch, tok, dim = hidden.shape
    rows = n_batch * tok
    inner, n_state = a_log.shape
    wq_t = w_q.transpose(1, 2, 0).reshape(-1, dim)
    wk_t = w_k.transpose(1, 2, 0).reshape(-1, dim)
    wv_t = w_v.transpose(1, 2, 0).reshape(-1, dim)
    kv_dim = wk_t.shape[0]
    wo = w_o.reshape(-1, dim)
    wxp = w_xproj.T
    vm = pl.BlockSpec(memory_space=pltpu.VMEM)
    hbm = pl.BlockSpec(memory_space=pl.ANY)
    peers = max(n_dev - 1, 1)
    per = n_batch // n_dev
    lanes = inner // 128
    params = dict(vmem_limit_bytes=63 * 1024 * 1024)
    if n_dev > 1:
        params.update(collective_id=0, has_side_effects=True)
    return pl.pallas_call(
        functools.partial(layer_kernel, n_dev, axis),
        out_shape=jax.ShapeDtypeStruct(hidden.shape, BF16),
        in_specs=[hbm] + [vm] * 11 + [hbm] * 12,
        out_specs=hbm,
        scratch_shapes=[
            pltpu.VMEM((NS, dim, CH), BF16),
            pltpu.VMEM((2 * kv_dim, dim), BF16),
            pltpu.VMEM(wxp.shape, BF16),
            pltpu.VMEM(w_dt.shape, BF16),
            pltpu.VMEM((rows, dim), BF16),
            pltpu.VMEM((rows, dim), BF16),
            pltpu.VMEM((rows, dim), BF16),
            pltpu.VMEM((rows, 2 * kv_dim), BF16),
            pltpu.VMEM((rows, dim), F32),
            pltpu.VMEM((rows, dim), BF16),
            pltpu.VMEM((2, rows + 8 * per, CH), F32),
            pltpu.VMEM((rows, inner), BF16),
            pltpu.VMEM((rows, inner), BF16),
            pltpu.VMEM((2 * n_state, rows, 128), F32),
            pltpu.VMEM((lanes * ST, 128), F32),
            pltpu.VMEM((lanes * ST, 128), F32),
            pltpu.VMEM((8 * (rows // per + 4), 128), F32),
            pltpu.VMEM((n_state * SA, 128), F32),
            pltpu.SemaphoreType.DMA((NS,)),
            pltpu.SemaphoreType.DMA((4,)),
            pltpu.SemaphoreType.DMA((peers, per)),
            pltpu.SemaphoreType.DMA((peers, per)),
            pltpu.SemaphoreType.DMA,
            pltpu.SemaphoreType.DMA,
            pltpu.SemaphoreType.DMA((per, dim // CH + 1)),
        ],
        compiler_params=pltpu.CompilerParams(**params),
        cost_estimate=pl.CostEstimate(flops=45_000_000_000, bytes_accessed=180_000_000, transcendentals=20_000_000),
        name="layers",
    )(hidden, attn_norm, mlp_norm, mamba_norm, conv_w, conv_b, dt_norm, b_norm, c_norm, dt_bias, d_skip, a_log.T,
      wq_t, wk_t, wv_t, wo, w_gate, w_up, w_down, w_in_x, w_in_z, wxp, w_dt, w_out)


def solution(mesh):
    act_spec = P("dp", "sp", None)
    return jax.shard_map(
        functools.partial(local_layers, mesh.shape["sp"], "sp"),
        mesh=mesh,
        in_specs=(act_spec,) + (P(),) * 23,
        out_specs=act_spec,
        check_vma=False,
    )
```

time: 148 us -> 125 us (0.84)
  blocking collectives: 18.6 us -> 0 us
  Pallas kernels: 104 us -> 122 us
  waiting for transfers between devices: 7.7 us -> 0 us
  starting transfers between devices: 6.01 us -> 0 us
  other arithmetic: 4.88 us -> 0 us
  local copies, waits for them, and re-layouts: 5.46 us -> 2.3 us
    all_to_all x1 -> x0, blocking collectives: 18.6 us -> none  [group_layers(): return lax.all_to_all(done, 'sp', 0, 0).reshape(n_batch, tok, dim)]
    pallas_call x1, Pallas kernels: 104 us -> 122 us  [local_layers(): pl.pallas_call(functools.partial(layer_kernel, n_dev, axis), out_shape=ja...]
    all_to_all x1 -> x0, waiting for transfers between devices: 7.7 us -> none  [group_layers(): seq = lax.all_to_all(hidden.reshape(n_shards, per, tok, dim), 'sp', 0, 0)]
    all_to_all x1 -> x0, starting transfers between devices: 6.01 us -> none  [group_layers(): seq = lax.all_to_all(hidden.reshape(n_shards, per, tok, dim), 'sp', 0, 0)]
    unnamed x5 -> x0, other arithmetic: 3.53 us -> none
    reshape x2 -> x0, local copies, waits for them, and re-layouts: 2 us -> none  [the longest x1 1.29 us: group_layers(): done = done.reshape(per, n_shards, tok, dim).transpose(1, 0, 2, 3)]
  transfers between devices with their start and end apart: 1 -> 0, of which waited for: 1 -> 0; matrix products, arithmetic and copies ran while one was open for 5% -> 0% of each run, Pallas kernels for 0% -> 0%
where the time goes in v2:
time: 125 us
  Pallas kernels  122 us (98%)
  local copies, waits for them, and re-layouts  2.3 us (2%)
    pallas_call x1, Pallas kernels, local_layers(): pl.pallas_call(functools.partial(layer_kernel, n_dev, axis), out_shape=ja...  122 us

profile of v2, /device:TPU:81, one launch (start us, length us, event | category | flops | bytes accessed | tf_op | source)
XLA Modules:
  0.0 124.6 jit_solution(561251262321678511)
XLA Ops:
  0.0 122.3 %layers.1 = bf16[16,16,2048]{2,1,0:T(8,128)(2,1)} custom-call(bf16[16,16,2048]{2,1,0:T(8,128)(2,1)} %x_in.1, bf16[2048]{0:T(1024)(128)(2,1)} %attn_norm.1, bf16[2048]{0:T(1024)(128)(2,1)} %mlp_norm.1, bf16[2048]{0:T(1024)(128)(2,1)} %mamba_norm.1, bf16[4,4096]{1,0:T(4,128)(2,1)} %conv_w.1, bf16[4096]{0:T(1024)(128)(2,1)} %conv_b.1, f32[128]{0:T(128)} %dt_norm.1, ...), custom_call_target="tpu_custom_call" | custom-call | flops 44999999488 | bytes 180000000 | tf_op jit(solution)/shard_map/layers/pallas_call | solution.py:441
  122.3 2.3 %copy.26 = bf16[16,16,2048]{2,1,0:T(8,128)(2,1)} copy(bf16[16,16,2048]{2,1,0:T(8,128)(2,1)} %layers.1) | data formatting | bytes 2097152

commit v3 on v2

--- a/solution.py
+++ b/solution.py
@@ -43,13 +43,14 @@
     n_dev, axis, x_in, attn_norm, mlp_norm, mamba_norm, conv_w, conv_b, dt_norm, b_norm, c_norm, dt_bias, d_skip, alog,
     wq, wk, wv, wo, wg, wu, wd, wix, wiz, wxp, wdt, wout,
     out, ring, kvw, xpw, dtw, hid, norm, q, kv, acc, res, xpad, conv, zg, bc, dl, dc, ys, amat,
-    sem, sem2, in_send, in_recv, out_send, out_recv, own_sem,
+    spare, sem, sem2, sem3, in_send, in_recv, out_send, out_recv, own_sem,
 ):
     n_batch, tok, dim = x_in.shape
     per = n_batch // n_dev
     seq = tok * n_dev
     rows = per * seq
-    inner = conv.shape[1]
+    inner = wix.shape[1]
+    chunks = inner // CH
     n_state = alog.shape[0]
     rank = wdt.shape[0]
     me = lax.axis_index(axis) if n_dev > 1 else 0
@@ -67,6 +68,14 @@
 
     def block(w, k, c, slot):
         return pltpu.make_async_copy(w.at[pl.ds(k * dim, dim), pl.ds(c * CH, CH)], ring.at[slot], sem.at[slot])
+
+    early = [spare.at[0], spare.at[1], conv, zg]
+
+    def first_down(n):
+        return pltpu.make_async_copy(wd.at[pl.ds(0, dim), pl.ds(n * CH, CH)], early[n], sem3.at[n])
+
+    def piece(e, b):
+        return pl.ds(pl.multiple_of(e * rows + b * seq, seq), seq)
 
     def ready(slot):
         pltpu.make_async_copy(wg.at[:, pl.ds(0, CH)], ring.at[slot], sem.at[slot]).wait()
@@ -119,15 +128,24 @@
     cols(wu, 0, 9).start()
     cols(wg, 1, 10).start()
     cols(wu, 1, 11).start()
+    for n in range(4):
+        first_down(n).start()
     xp_load.start()
     dt_load.start()
 
-    def normalize(src, gain_ref, start=0, count=rows):
+    def normalize(src, gain_ref, start=0, count=rows, keep=None):
         gain = gain_ref[...].astype(F32).reshape(1, dim)
 
         def body(i, _):
             r = pl.ds(pl.multiple_of(start + i * 16, 16), 16)
-            norm[r, :] = (rms(src[r, :].astype(F32)) * gain).astype(BF16)
+            v = src[r, :]
+            if keep is not None:
+                v = v.astype(BF16)
+                keep[r, :] = v
+            v = v.astype(F32)
+            if keep is not None:
+                src[r, :] = v
+            norm[r, :] = (rms(v) * gain).astype(BF16)
             return 0
 
         lax.fori_loop(0, count // 16, body, 0, unroll=2)
@@ -179,7 +197,12 @@
             v_load.wait()
         kv[rb, :] = nt_dot(norm[rb, :], kvw[...]).astype(BF16)
 
-        def attend(m, _, rb=rb):
+        def attend(it, _, rb=rb):
+            for m in (2 * it, 2 * it + 1):
+                attend_tile(m, rb)
+            return 0
+
+        def attend_tile(m, rb):
             kt = kv[rb, pl.ds(pl.multiple_of(m * 128, 128), 128)].astype(F32)
             vt = kv[rb, pl.ds(pl.multiple_of(CH + m * 128, 128), 128)].astype(F32)
             for par in range(2):
@@ -196,102 +219,100 @@
                 o = nn_dot(jnp.concatenate(ps, axis=1), v2).astype(BF16)
                 norm[rb, pl.ds(c0, 128)] = o[:seq]
                 norm[rb, pl.ds(c0 + 128, 128)] = o[seq:]
-            return 0
-
-        lax.fori_loop(0, pairs, attend, 0)
+
+        lax.fori_loop(0, pairs // 2, attend, 0)
 
     def out_proj(n, _):
         ready(4 + n)
         c = pl.ds(pl.multiple_of(n * CH, CH), CH)
-        res[:, c] = (hid[:, c].astype(F32) + nn_dot(norm[...], ring[4 + n])).astype(BF16)
-        block(wd, 0, n, 4 + n).start()
+        h1 = (hid[:, c].astype(F32) + nn_dot(norm[...], ring[4 + n])).astype(BF16)
+        res[:, c] = h1
+        acc[:, c] = h1.astype(F32)
+        block(wd, 1, n, 4 + n).start()
         return 0
 
     lax.fori_loop(0, 4, out_proj, 0)
 
     normalize(res, mlp_norm)
 
+    def up(i, s):
+        slots = [slot_of(4 * i + p) for p in range(4)]
+        for sl in slots:
+            ready(sl)
+        for p in range(2):
+            gate = nn_dot(norm[...], ring[slots[2 * p]])
+            upv = nn_dot(norm[...], ring[slots[2 * p + 1]])
+            act[:, pl.ds(pl.multiple_of((2 * i + p) * CH, CH), CH)] = (silu(gate) * upv).astype(BF16)
+
+        @pl.when(s < 3)
+        def _():
+            for p in range(2):
+                cols(wg, 4 * (s + 1) + 2 * i + p, slots[2 * p]).start()
+                cols(wu, 4 * (s + 1) + 2 * i + p, slots[2 * p + 1]).start()
+
+        @pl.when(s == 3)
+        def _():
+            for p in range(4):
+                cols(wix, 4 * i + p, slots[p]).start()
+
+        return s
+
+    lax.fori_loop(0, 2, up, jnp.int32(0))
+    for n in range(4):
+        first_down(n).wait()
+    for n in range(4):
+        acc[:, n * CH:(n + 1) * CH] += nn_dot(act[...], early[n][...])
+
     def mlp(s, _):
-        def up(n, _):
-            sg = slot_of(2 * n)
-            su = slot_of(2 * n + 1)
-            ready(sg)
-            ready(su)
-            gate = nn_dot(norm[...], ring[sg])
-            upv = nn_dot(norm[...], ring[su])
-            act[:, pl.ds(pl.multiple_of(n * CH, CH), CH)] = (silu(gate) * upv).astype(BF16)
-
-            @pl.when(s < 3)
-            def _():
-                cols(wg, 4 * (s + 1) + n, sg).start()
-                cols(wu, 4 * (s + 1) + n, su).start()
-
-            @pl.when(s == 3)
-            def _():
-                cols(wix, 2 * n, sg).start()
-                cols(wix, 2 * n + 1, su).start()
-
-            return 0
-
-        lax.fori_loop(0, 4, up, 0)
-
-        def down(n, _):
-            sd = slot_of(8 + n)
-            ready(sd)
-            c = pl.ds(pl.multiple_of(n * CH, CH), CH)
-            term = nn_dot(act[...], ring[sd])
-
-            @pl.when(s == 0)
-            def _():
-                acc[:, c] = res[:, c].astype(F32) + term
-
-            @pl.when((s > 0) & (s < 3))
-            def _():
-                acc[:, c] += term
-
-            @pl.when(s == 3)
-            def _():
-                res[:, c] = (acc[:, c] + term).astype(BF16)
-
-            @pl.when(s < 3)
-            def _():
-                block(wd, s + 1, n, sd).start()
-
-            @pl.when(s == 3)
-            def _():
-                cols(wiz, n, sd).start()
-
-            return 0
-
-        lax.fori_loop(0, 4, down, 0)
+        lax.fori_loop(0, 2, up, s)
+        for n in range(4):
+            ready((16 + n) % NS)
+        for n in range(4):
+            acc[:, n * CH:(n + 1) * CH] += nn_dot(act[...], ring[(16 + n) % NS])
+
+        @pl.when(s < 3)
+        def _():
+            for n in range(4):
+                block(wd, s + 1, n, (16 + n) % NS).start()
+
+        @pl.when(s == 3)
+        def _():
+            for n in range(4):
+                cols(wiz, n, (16 + n) % NS).start()
+
         return 0
 
-    lax.fori_loop(0, 4, mlp, 0)
-
-    normalize(res, mamba_norm)
+    lax.fori_loop(1, 4, mlp, 0)
+
+    normalize(acc, mamba_norm, 0, rows, res)
     pitch = seq + 8
+    tiles = CH // 128
     for i in range(2):
-        for b in range(per):
-            xpad[i, pl.ds(b * pitch, 8), :] = jnp.zeros((8, CH), F32)
+        for b in range(per * tiles):
+            xpad[i, pl.ds(b * pitch, 8), :] = jnp.zeros((8, 128), F32)
 
     def conv_chunk(e):
         i = lax.rem(e, 2)
-        c = pl.ds(pl.multiple_of(e * CH, CH), CH)
-        bias = conv_b[c].astype(F32).reshape(1, CH)
-        taps = [conv_w[j:j + 1, c].astype(F32) for j in range(CONV)]
-        for b in range(per):
-            v = bias
-            for j in range(CONV):
-                v = v + xpad[i, pl.ds(b * pitch + 8 - (CONV - 1) + j, seq), :] * taps[j]
-            conv[pl.ds(b * seq, seq), c] = silu(v).astype(BF16)
+        whole = conv_b[pl.ds(pl.multiple_of(e * CH, CH), CH)].astype(F32).reshape(1, CH)
+        for j in range(tiles):
+            c = pl.ds(pl.multiple_of(e * CH + j * 128, 128), 128)
+            bias = whole[:, j * 128:(j + 1) * 128]
+            taps = [conv_w[k:k + 1, c].astype(F32) for k in range(CONV)]
+            for b in range(per):
+                v = bias
+                for k in range(CONV):
+                    v = v + xpad[i, pl.ds((j * per + b) * pitch + 8 - (CONV - 1) + k, seq), :] * taps[k]
+                conv[piece(e, b), j * 128:(j + 1) * 128] = silu(v).astype(BF16)
 
     def inx(e, _):
         sl = slot_of(e)
         ready(sl)
         conv_chunk(jnp.maximum(e - 1, 0))
         xi = nn_dot(norm[...], ring[sl]).astype(BF16).astype(F32)
-        for b in range(per):
-            xpad[lax.rem(e, 2), pl.ds(b * pitch + 8, seq), :] = xi[b * seq:(b + 1) * seq]
+        for j in range(tiles):
+            for b in range(per):
+                xpad[lax.rem(e, 2), pl.ds((j * per + b) * pitch + 8, seq), :] = (
+                    xi[b * seq:(b + 1) * seq, j * 128:(j + 1) * 128])
 
         @pl.when(e < 4)
         def _():
@@ -303,12 +324,12 @@
 
         return 0
 
-    lax.fori_loop(0, inner // CH, inx, 0)
-    conv_chunk(jnp.int32(inner // CH - 1))
+    lax.fori_loop(0, chunks, inx, 0)
+    conv_chunk(jnp.int32(chunks - 1))
 
     xp_load.wait()
     dt_load.wait()
-    r = nt_dot(conv[...], xpw[...])
+    r = nt_dot(jnp.concatenate([conv[e * rows:(e + 1) * rows, :] for e in range(chunks)], axis=1), xpw[...])
     dt_in = (rms(r[:, :rank]) * dt_norm[...].reshape(1, rank)).astype(BF16)
     bm = rms(r[:, rank:rank + n_state]) * b_norm[...].reshape(1, n_state)
     cm = rms(r[:, rank + n_state:rank + 2 * n_state]) * c_norm[...].reshape(1, n_state)
@@ -317,17 +338,17 @@
         bc[n_state + n] = jnp.broadcast_to(cm[:, n:n + 1], (rows, 128))
     kv[:, :rank] = dt_in
 
-    def inz(e, _):
+    def deltas(e, _):
+        c = pl.ds(pl.multiple_of(e * CH, CH), CH)
+        step = softplus(nn_dot(kv[:, :rank], dtw[:, c]) + dt_bias[c].reshape(1, CH))
+        prod = step * conv[pl.ds(pl.multiple_of(e * rows, rows), rows), :].astype(F32)
+        for j in range(tiles):
+            at = pl.ds((e * tiles + j) * ST, rows)
+            dl[at, :] = step[:, j * 128:(j + 1) * 128]
+            dc[at, :] = prod[:, j * 128:(j + 1) * 128]
         sl = slot_of(8 + e)
         ready(sl)
-        c = pl.ds(pl.multiple_of(e * CH, CH), CH)
-        step = softplus(nn_dot(kv[:, :rank], dtw[:, c]) + dt_bias[c].reshape(1, CH))
-        prod = step * conv[:, c].astype(F32)
-        for j in range(CH // 128):
-            at = pl.ds((e * (CH // 128) + j) * ST, rows)
-            dl[at, :] = step[:, j * 128:(j + 1) * 128]
-            dc[at, :] = prod[:, j * 128:(j + 1) * 128]
-        zg[:, c] = nn_dot(norm[...], ring[sl]).astype(BF16)
+        zg[pl.ds(pl.multiple_of(e * rows, rows), rows), :] = nn_dot(norm[...], ring[sl]).astype(BF16)
 
         @pl.when(e < 4)
         def _():
@@ -335,13 +356,16 @@
 
         return 0
 
-    lax.fori_loop(0, inner // CH, inz, 0)
+    lax.fori_loop(0, chunks, deltas, 0)
+
+    def chunk_cols(n):
+        return pl.ds(n * CH, CH) if isinstance(n, int) else pl.ds(pl.multiple_of(n * CH, CH), CH)
 
     def send_out(k, b, n):
         to = peer_of(k)
         return pltpu.make_async_remote_copy(
-            src_ref=q.at[pl.ds(pl.multiple_of(b * seq + to * tok, tok), tok), pl.ds(n * CH, CH)],
-            dst_ref=out.at[me * per + b, :, pl.ds(n * CH, CH)],
+            src_ref=q.at[pl.ds(pl.multiple_of(b * seq + to * tok, tok), tok), chunk_cols(n)],
+            dst_ref=out.at[me * per + b, :, chunk_cols(n)],
             send_sem=out_send,
             recv_sem=out_recv,
             device_id={axis: to},
@@ -350,10 +374,26 @@
 
     def own_out(b, n):
         return pltpu.make_async_copy(
-            q.at[pl.ds(pl.multiple_of(b * seq + me * tok, tok), tok), pl.ds(n * CH, CH)],
-            out.at[me * per + b, :, pl.ds(n * CH, CH)],
+            q.at[pl.ds(pl.multiple_of(b * seq + me * tok, tok), tok), chunk_cols(n)],
+            out.at[me * per + b, :, chunk_cols(n)],
             own_sem.at[b, n],
         )
+
+    n_part = 4
+    part = seq // n_part
+    deep = inner // n_part
+
+    def send_chunk(b, n):
+        own_out(b, n).start()
+        if n_dev > 1:
+            for k in order:
+                send_out(k, b, n).start()
+
+    def out_matmul(blk, i):
+        lhs = jnp.concatenate([zg[piece(i * (deep // CH) + p, 0), :] for p in range(deep // CH)], axis=1)
+        to = pl.ds(pl.multiple_of(blk * CH, CH), CH)
+        at = pl.ds(pl.multiple_of(lax.rem(i, 2) * deep, deep), deep)
+        acc[:seq, to] += nn_dot(lhs, ring[slot_of(4 + 2 * blk + lax.div(i, 2)), at, :])
 
     for b in range(per):
         rb = pl.ds(b * seq, seq)
@@ -361,8 +401,11 @@
         def scan_block(blk, _, b=b, rb=rb):
             base = blk * (8 * ST) + b * seq
             a_rows = [amat[pl.ds(n * SA + blk * 8, 8), :] for n in range(n_state)]
-
-            def step_fn(t, hs):
+            if b == 1:
+                ready(slot_of(4 + 2 * blk))
+                ready(slot_of(5 + 2 * blk))
+
+            def step(t, hs):
                 at = pl.ds(base + t, 8, stride=ST)
                 d = dl[at, :]
                 x = dc[at, :]
@@ -377,28 +420,42 @@
                 ys[pl.ds(t, 8, stride=seq + 4), :] = y
                 return tuple(new)
 
-            lax.fori_loop(0, seq, step_fn, tuple(jnp.zeros((8, 128), F32) for _ in range(n_state)), unroll=4)
+            def scan_part(i, hs):
+                out_matmul(blk, i)
+                for u in range(part):
+                    hs = step(i * part + u, hs)
+                return hs
+
+            zero = tuple(jnp.zeros((8, 128), F32) for _ in range(n_state))
+            if b == 1:
+                lax.fori_loop(0, n_part, scan_part, zero)
+            else:
+                lax.fori_loop(0, seq, step, zero, unroll=8)
+            if b == 1:
+                c = pl.ds(pl.multiple_of(blk * CH, CH), CH)
+                q[:seq, c] = acc[:seq, c].astype(BF16)
             for j in range(8):
                 c = pl.ds(pl.multiple_of(blk * 1024 + j * 128, 128), 128)
-                y = ys[pl.ds(j * (seq + 4), seq), :] + d_skip[c].reshape(1, 128) * conv[rb, c].astype(F32)
-                zg[rb, c] = (y * silu(zg[rb, c].astype(F32))).astype(BF16)
+                at = (piece(2 * blk + j // tiles, b), slice(j % tiles * 128, (j % tiles + 1) * 128))
+                y = ys[pl.ds(j * (seq + 4), seq), :] + d_skip[c].reshape(1, 128) * conv[at].astype(F32)
+                zg[at] = (y * silu(zg[at].astype(F32))).astype(BF16)
+            if b == 1:
+                send_chunk(0, blk)
             return 0
 
         lax.fori_loop(0, inner // 1024, scan_block, 0)
 
-        for n in range(dim // CH):
-            s0 = (4 + 2 * n + 8) % NS
-            s1 = (5 + 2 * n + 8) % NS
-            if b == 0:
-                ready(s0)
-                ready(s1)
-            c = slice(n * CH, (n + 1) * CH)
-            y = nn_dot(zg[rb, :dim], ring[s0]) + nn_dot(zg[rb, dim:], ring[s1])
-            q[rb, c] = (res[rb, c].astype(F32) + y).astype(BF16)
-            own_out(b, n).start()
-            if n_dev > 1:
-                for k in order:
-                    send_out(k, b, n).start()
+    last = per - 1
+    rb = pl.ds(last * seq, seq)
+    lhs = [zg[piece(e, last), :] for e in range(chunks)]
+    for n in range(dim // CH):
+        s0 = (4 + 2 * n + 8) % NS
+        s1 = (5 + 2 * n + 8) % NS
+        c = slice(n * CH, (n + 1) * CH)
+        y = (nn_dot(jnp.concatenate(lhs[:chunks // 2], axis=1), ring[s0])
+             + nn_dot(jnp.concatenate(lhs[chunks // 2:], axis=1), ring[s1]))
+        q[rb, c] = (res[rb, c].astype(F32) + y).astype(BF16)
+        send_chunk(last, n)
 
     for b in range(per):
         for n in range(dim // CH):
@@ -454,15 +511,17 @@
             pltpu.VMEM((rows, 2 * kv_dim), BF16),
             pltpu.VMEM((rows, dim), F32),
             pltpu.VMEM((rows, dim), BF16),
-            pltpu.VMEM((2, rows + 8 * per, CH), F32),
-            pltpu.VMEM((rows, inner), BF16),
-            pltpu.VMEM((rows, inner), BF16),
+            pltpu.VMEM((2, (rows + 8 * per) * (CH // 128), 128), F32),
+            pltpu.VMEM((dim, CH), BF16),
+            pltpu.VMEM((dim, CH), BF16),
             pltpu.VMEM((2 * n_state, rows, 128), F32),
             pltpu.VMEM((lanes * ST, 128), F32),
             pltpu.VMEM((lanes * ST, 128), F32),
             pltpu.VMEM((8 * (rows // per + 4), 128), F32),
             pltpu.VMEM((n_state * SA, 128), F32),
+            pltpu.VMEM((2, dim, CH), BF16),
             pltpu.SemaphoreType.DMA((NS,)),
+            pltpu.SemaphoreType.DMA((4,)),
             pltpu.SemaphoreType.DMA((4,)),
             pltpu.SemaphoreType.DMA((peers, per)),
             pltpu.SemaphoreType.DMA((peers, per)),

time: 125 us -> 117 us (0.936)
  Pallas kernels: 122 us -> 115 us
    pallas_call x1, Pallas kernels: 122 us -> 115 us  [local_layers(): pl.pallas_call(functools.partial(layer_kernel, n_dev, axis), out_shape=ja...]
where the time goes in v3:
time: 117 us
  Pallas kernels  115 us (98%)
  local copies, waits for them, and re-layouts  2.3 us (2%)
    pallas_call x1, Pallas kernels, local_layers(): pl.pallas_call(functools.partial(layer_kernel, n_dev, axis), out_shape=ja...  115 us

profile of v3, /device:TPU:81, one launch (start us, length us, event | category | flops | bytes accessed | tf_op | source)
XLA Modules:
  0.0 117.1 jit_solution(8426372158961259539)
XLA Ops:
  0.0 114.8 %layers.1 = bf16[16,16,2048]{2,1,0:T(8,128)(2,1)} custom-call(bf16[16,16,2048]{2,1,0:T(8,128)(2,1)} %x_in.1, bf16[2048]{0:T(1024)(128)(2,1)} %attn_norm.1, bf16[2048]{0:T(1024)(128)(2,1)} %mlp_norm.1, bf16[2048]{0:T(1024)(128)(2,1)} %mamba_norm.1, bf16[4,4096]{1,0:T(4,128)(2,1)} %conv_w.1, bf16[4096]{0:T(1024)(128)(2,1)} %conv_b.1, f32[128]{0:T(128)} %dt_norm.1, ...), custom_call_target="tpu_custom_call" | custom-call | flops 44999999488 | bytes 180000000 | tf_op jit(solution)/shard_map/layers/pallas_call | solution.py:498
  114.8 2.3 %copy.26 = bf16[16,16,2048]{2,1,0:T(8,128)(2,1)} copy(bf16[16,16,2048]{2,1,0:T(8,128)(2,1)} %layers.1) | data formatting | bytes 2097152

commit v4 on v3

--- a/solution.py
+++ b/solution.py
@@ -291,8 +291,7 @@
         for b in range(per * tiles):
             xpad[i, pl.ds(b * pitch, 8), :] = jnp.zeros((8, 128), F32)
 
-    def conv_chunk(e):
-        i = lax.rem(e, 2)
+    def conv_chunk(e, i):
         whole = conv_b[pl.ds(pl.multiple_of(e * CH, CH), CH)].astype(F32).reshape(1, CH)
         for j in range(tiles):
             c = pl.ds(pl.multiple_of(e * CH + j * 128, 128), 128)
@@ -304,28 +303,39 @@
                     v = v + xpad[i, pl.ds((j * per + b) * pitch + 8 - (CONV - 1) + k, seq), :] * taps[k]
                 conv[piece(e, b), j * 128:(j + 1) * 128] = silu(v).astype(BF16)
 
-    def inx(e, _):
-        sl = slot_of(e)
-        ready(sl)
-        conv_chunk(jnp.maximum(e - 1, 0))
-        xi = nn_dot(norm[...], ring[sl]).astype(BF16).astype(F32)
+    def in_matmul(sl):
+        return nn_dot(norm[...], ring[sl]).astype(BF16).astype(F32)
+
+    def keep_xi(i, xi):
         for j in range(tiles):
             for b in range(per):
-                xpad[lax.rem(e, 2), pl.ds((j * per + b) * pitch + 8, seq), :] = (
-                    xi[b * seq:(b + 1) * seq, j * 128:(j + 1) * 128])
-
-        @pl.when(e < 4)
+                xpad[i, pl.ds((j * per + b) * pitch + 8, seq), :] = xi[b * seq:(b + 1) * seq, j * 128:(j + 1) * 128]
+
+    def inx(p, _):
+        s0 = slot_of(2 * p)
+        s1 = slot_of(2 * p + 1)
+        ready(s0)
+        ready(s1)
+        conv_chunk(jnp.maximum(2 * p - 1, 0), 1)
+        keep_xi(0, in_matmul(s0))
+        xi = in_matmul(s1)
+        conv_chunk(2 * p, 0)
+        keep_xi(1, xi)
+
+        @pl.when(p < 2)
         def _():
-            cols(wiz, 4 + e, sl).start()
-
-        @pl.when(e >= 4)
+            cols(wiz, 4 + 2 * p, s0).start()
+            cols(wiz, 5 + 2 * p, s1).start()
+
+        @pl.when(p >= 2)
         def _():
-            block(wout, lax.rem(e, 2), lax.div(e - 4, 2), sl).start()
+            block(wout, 0, p - 2, s0).start()
+            block(wout, 1, p - 2, s1).start()
 
         return 0
 
-    lax.fori_loop(0, chunks, inx, 0)
-    conv_chunk(jnp.int32(chunks - 1))
+    lax.fori_loop(0, chunks // 2, inx, 0)
+    conv_chunk(jnp.int32(chunks - 1), 1)
 
     xp_load.wait()
     dt_load.wait()
@@ -333,30 +343,32 @@
     dt_in = (rms(r[:, :rank]) * dt_norm[...].reshape(1, rank)).astype(BF16)
     bm = rms(r[:, rank:rank + n_state]) * b_norm[...].reshape(1, n_state)
     cm = rms(r[:, rank + n_state:rank + 2 * n_state]) * c_norm[...].reshape(1, n_state)
-    for n in range(n_state):
-        bc[n] = jnp.broadcast_to(bm[:, n:n + 1], (rows, 128))
-        bc[n_state + n] = jnp.broadcast_to(cm[:, n:n + 1], (rows, 128))
     kv[:, :rank] = dt_in
-
-    def deltas(e, _):
-        c = pl.ds(pl.multiple_of(e * CH, CH), CH)
+    per_pair = 2 * n_state // chunks
+
+    def deltas(e):
+        c = slice(e * CH, (e + 1) * CH)
         step = softplus(nn_dot(kv[:, :rank], dtw[:, c]) + dt_bias[c].reshape(1, CH))
-        prod = step * conv[pl.ds(pl.multiple_of(e * rows, rows), rows), :].astype(F32)
+        prod = step * conv[e * rows:(e + 1) * rows, :].astype(F32)
         for j in range(tiles):
             at = pl.ds((e * tiles + j) * ST, rows)
             dl[at, :] = step[:, j * 128:(j + 1) * 128]
             dc[at, :] = prod[:, j * 128:(j + 1) * 128]
-        sl = slot_of(8 + e)
-        ready(sl)
-        zg[pl.ds(pl.multiple_of(e * rows, rows), rows), :] = nn_dot(norm[...], ring[sl]).astype(BF16)
-
-        @pl.when(e < 4)
-        def _():
-            block(wout, lax.rem(e, 2), 2 + lax.div(e, 2), sl).start()
-
-        return 0
-
-    lax.fori_loop(0, chunks, deltas, 0)
+
+    for p in range(chunks // 2):
+        slots = [(16 + 2 * p + k) % NS for k in range(2)]
+        for sl in slots:
+            ready(sl)
+        for k in range(2):
+            e = 2 * p + k
+            zg[e * rows:(e + 1) * rows, :] = nn_dot(norm[...], ring[slots[k]]).astype(BF16)
+            deltas(e)
+        for n in range(p * per_pair, (p + 1) * per_pair):
+            bc[n] = jnp.broadcast_to(bm[:, n:n + 1], (rows, 128))
+            bc[n_state + n] = jnp.broadcast_to(cm[:, n:n + 1], (rows, 128))
+        if p < 2:
+            for k in range(2):
+                block(wout, k, 2 + p, slots[k]).start()
 
     def chunk_cols(n):
         return pl.ds(n * CH, CH) if isinstance(n, int) else pl.ds(pl.multiple_of(n * CH, CH), CH)

time: 117 us -> 113 us (0.966)
  Pallas kernels: 115 us -> 111 us
    pallas_call x1, Pallas kernels: 115 us -> 111 us  [local_layers(): pl.pallas_call(functools.partial(layer_kernel, n_dev, axis), out_shape=ja...]
where the time goes in v4:
time: 113 us
  Pallas kernels  111 us (98%)
  local copies, waits for them, and re-layouts  2.3 us (2%)
    pallas_call x1, Pallas kernels, local_layers(): pl.pallas_call(functools.partial(layer_kernel, n_dev, axis), out_shape=ja...  111 us
    unnamed x1, local copies, waits for them, and re-layouts  2.3 us

profile of v4, /device:TPU:81, one launch (start us, length us, event | category | flops | bytes accessed | tf_op | source)
XLA Modules:
  0.0 112.9 jit_solution(14341389489303128014)
XLA Ops:
  0.0 110.6 %layers.1 = bf16[16,16,2048]{2,1,0:T(8,128)(2,1)} custom-call(bf16[16,16,2048]{2,1,0:T(8,128)(2,1)} %x_in.1, bf16[2048]{0:T(1024)(128)(2,1)} %attn_norm.1, bf16[2048]{0:T(1024)(128)(2,1)} %mlp_norm.1, bf16[2048]{0:T(1024)(128)(2,1)} %mamba_norm.1, bf16[4,4096]{1,0:T(4,128)(2,1)} %conv_w.1, bf16[4096]{0:T(1024)(128)(2,1)} %conv_b.1, f32[128]{0:T(128)} %dt_norm.1, ...), custom_call_target="tpu_custom_call" | custom-call | flops 44999999488 | bytes 180000000 | tf_op jit(solution)/shard_map/layers/pallas_call | solution.py:510
  110.6 2.3 %copy.26 = bf16[16,16,2048]{2,1,0:T(8,128)(2,1)} copy(bf16[16,16,2048]{2,1,0:T(8,128)(2,1)} %layers.1) | data formatting | bytes 2097152
